TPU v7x, 128 devices: a whole 4x4x4 slice. The times are simulated.
128 devices in a mesh: seq: 32 (over z, y, core), head: 4 (over x).
Axes of the slice: x: 4, y: 4, z: 4, core: 2. Of those that a mesh axis runs over, the one named last changes fastest.
Arguments:
- tokens: bfloat16 [16384, 2560], P('seq'), may hold values from -6 to 6
- proj_inner: bfloat16 [2560, 5120], P(None, 'head'), may hold values from -0.125 to 0.125
- proj_gate: bfloat16 [2560, 5120], P(None, 'head'), may hold values from -0.125 to 0.125
- proj_bc: bfloat16 [2560, 256], replicated, may hold values from -0.03125 to 0.03125
- proj_step: bfloat16 [2560, 80], P(None, 'head'), may hold values from -0.125 to 0.125
- conv_inner: float32 [4, 5120], P(None, 'head'), may hold values from -3 to 3
- conv_bc: float32 [4, 256], replicated, may hold values from -3 to 3
- offset_inner: float32 [5120], P('head'), may hold values from -3 to 3
- offset_bc: float32 [256], replicated, may hold values from -1.2 to 1.2
- step_bias: float32 [80], P('head'), as said below
- decay_log: float32 [80], P('head'), as said below
- skip_gain: float32 [80], P('head'), may hold values from 0.5 to 2
- norm_weight: float32 [5120], P('head'), may hold values from 0.25 to 1.75
- out_weight: bfloat16 [5120, 2560], P('head'), may hold values from -0.078125 to 0.078125
Outputs:
- layer_out: bfloat16 [16384, 2560], P(('seq', 'head'))
Inputs may be any that keep to these rules, and one draw needn't show every extreme that they name: step_bias holds one value for each head, the same for every token. decay_log holds one value for each head, the same for every token.
All inputs are finite; a program needn't handle non-finite values.
Results may differ from a plain program's by a relative error of at most 0.013.
Values may be sent and summed in bfloat16 or wider, within the bound.
A program may use at most 128 MiB of HBM per device.

v0:
```python
import jax
import jax.numpy as jnp
from jax import lax
from jax.sharding import Mesh
from jax.sharding import PartitionSpec as P

HEADS = 80
HEADDIM = 64
STATE = 128
KERNEL = 4
SPAN = 128
SEQ = ("seq_0", "seq_1", "seq_2")
SEQ_HEAD = ("seq_0", "seq_1", "seq_2", "head")


def passed_along(block, axis, distance):
    devices = range(lax.axis_size(axis))
    route = [(i - distance, i) for i in devices if i - distance in devices]
    return lax.ppermute(block, axis, route)


def neutral_like(x, identity):
    return jax.tree.map(
        lambda a, e: jnp.broadcast_to(jnp.asarray(e, a.dtype), a.shape), x, identity
    )


def carried_in(x, axes, combine, identity):
    before = start = neutral_like(x, identity)
    running = x
    for axis in reversed(axes):
        size, index = (lax.axis_size(axis), lax.axis_index(axis))
        pieces = jax.tree.map(lambda part: lax.all_gather(part, axis), running)
        inside, running = (start, start)
        for k in range(size):
            passed = k < index
            running = combine(running, jax.tree.map(lambda part: part[k], pieces))
            inside = jax.tree.map(lambda new, old: jnp.where(passed, new, old), running, inside)
        before = combine(inside, before)
    return before


def sent_to_all(x, axis):
    copies = jnp.broadcast_to(x, (lax.axis_size(axis), *x.shape))
    return lax.all_to_all(copies, axis, split_axis=0, concat_axis=0, tiled=True)


def taken_together(x, axis):
    return sent_to_all(x, axis).sum(axis=0)


def in_blocks(x, dim, size):
    before, after = (x.shape[:dim], x.shape[dim + 1 :])
    return jnp.moveaxis(x.reshape(*before, size, -1, *after), dim, 0)


def summed_on_arrival(x, axis, dim):
    pieces = in_blocks(x, dim, lax.axis_size(axis))
    arrived = lax.all_to_all(pieces, axis, split_axis=0, concat_axis=0, tiled=True)
    return arrived.astype(jnp.float32).sum(axis=0)


def causal(padded, weight, offset, length):
    summed = jnp.zeros((length, weight.shape[1]), jnp.float32) + offset[None, :]
    for tap_index in range(weight.shape[0]):
        summed = summed + weight[tap_index][None, :] * padded[
            tap_index : tap_index + length
        ].astype(jnp.float32)
    return jax.nn.silu(summed).astype(jnp.bfloat16)


def combine_states(first_part, second_part):
    return (
        first_part[0] * second_part[0],
        second_part[0][:, None, None] * first_part[1] + second_part[1],
    )


def per_device(
    tokens,
    proj_inner,
    proj_gate,
    proj_bc,
    proj_step,
    conv_inner,
    conv_bc,
    offset_inner,
    offset_bc,
    step_bias,
    decay_log,
    skip_gain,
    norm_weight,
    out_weight,
):
    tok_rows = tokens.shape[0]
    head_count = step_bias.shape[0]
    inner_raw = jnp.dot(tokens, proj_inner, preferred_element_type=jnp.float32).astype(jnp.bfloat16)
    gate_raw = jnp.dot(tokens, proj_gate, preferred_element_type=jnp.float32).astype(jnp.bfloat16)
    bc_raw = jnp.dot(tokens, proj_bc, preferred_element_type=jnp.float32).astype(jnp.bfloat16)
    step_raw = jnp.dot(tokens, proj_step, preferred_element_type=jnp.float32)
    edge_inner, edge_bc = passed_along(
        (inner_raw[tok_rows - (KERNEL - 1) :], bc_raw[tok_rows - (KERNEL - 1) :]), SEQ, 1
    )
    inner_conv = causal(
        jnp.concatenate([edge_inner, inner_raw], 0), conv_inner, offset_inner, tok_rows
    )
    bc_conv = causal(jnp.concatenate([edge_bc, bc_raw], 0), conv_bc, offset_bc, tok_rows)
    step_sizes = jax.nn.softplus(step_raw + step_bias[None, :])
    log_decay = -jnp.exp(decay_log)[None, :] * step_sizes
    span_total = tok_rows // SPAN
    inner_blocks = inner_conv.reshape(span_total, SPAN, head_count, HEADDIM)
    write_blocks = bc_conv[:, :STATE].reshape(span_total, SPAN, STATE)
    read_blocks = bc_conv[:, STATE:].reshape(span_total, SPAN, STATE)
    step_blocks = step_sizes.reshape(span_total, SPAN, head_count)
    cumulative = jnp.cumsum(log_decay.reshape(span_total, SPAN, head_count), axis=1)
    scores = jnp.einsum(
        "cin,cjn->cij", read_blocks, write_blocks, preferred_element_type=jnp.float32
    )
    cum_t = jnp.swapaxes(cumulative, 1, 2)
    step_t = jnp.swapaxes(step_blocks, 1, 2)
    log_gaps = cum_t[:, :, :, None] - cum_t[:, :, None, :]
    causal_mask = jnp.tril(jnp.ones((SPAN, SPAN), bool))[None, None]
    decays = jnp.where(causal_mask, jnp.exp(jnp.where(causal_mask, log_gaps, 0.0)), 0.0)
    weights = (scores[:, None] * decays * step_t[:, :, None, :]).astype(jnp.bfloat16)
    intra_out = jnp.einsum(
        "chij,cjhp->cihp", weights, inner_blocks, preferred_element_type=jnp.float32
    )
    end_weights = jnp.exp(cumulative[:, -1:, :] - cumulative) * step_blocks
    local_states = jnp.einsum(
        "cjn,cjh,cjhp->chnp",
        write_blocks.astype(jnp.float32),
        end_weights,
        inner_blocks.astype(jnp.float32),
        precision=lax.Precision.HIGHEST,
    )
    span_decay = jnp.exp(cumulative[:, -1, :])
    read_wide = read_blocks.astype(jnp.float32)
    read_scale = jnp.exp(cumulative)[..., None]
    running = jnp.zeros((head_count, STATE, HEADDIM), jnp.float32)
    prior_states = []
    for number in range(span_total):
        prior_states.append(running)
        running = span_decay[number][:, None, None] * running + local_states[number]
    device_decay = jnp.prod(span_decay, axis=0)
    prefix_decay, incoming = carried_in(
        (device_decay, running),
        SEQ,
        combine_states,
        (jnp.ones_like(device_decay), jnp.zeros_like(running)),
    )
    inter_out = read_scale * jnp.einsum(
        "cin,chnp->cihp", read_wide, jnp.stack(prior_states), precision=lax.Precision.HIGHEST
    )
    leading_list = []
    product = jnp.ones((head_count,), jnp.float32)
    for number in range(span_total):
        leading_list.append(product)
        product = product * span_decay[number]
    leading = jnp.stack(leading_list)
    inter_out = inter_out + read_scale * leading[:, None, :, None] * jnp.einsum(
        "cin,hnp->cihp", read_wide, incoming, precision=lax.Precision.HIGHEST
    )
    mixed_out = (intra_out + inter_out).reshape(tok_rows, head_count, HEADDIM) + skip_gain[
        None, :, None
    ] * inner_conv.reshape(tok_rows, head_count, HEADDIM).astype(jnp.float32)
    gated_pre = mixed_out.reshape(tok_rows, head_count * HEADDIM) * jax.nn.silu(
        gate_raw.astype(jnp.float32)
    )
    squares = taken_together(jnp.sum(gated_pre * gated_pre, axis=1), "head")
    scale = 1.0 / jnp.sqrt(squares / (HEADS * HEADDIM) + 0.25)
    gated_out = (gated_pre * scale[:, None] * norm_weight[None, :]).astype(jnp.bfloat16)
    out_share = summed_on_arrival(
        jnp.dot(gated_out, out_weight, preferred_element_type=jnp.float32).astype(jnp.bfloat16),
        "head",
        0,
    )
    return out_share.astype(jnp.bfloat16)


def solution(mesh):
    torus = Mesh(
        mesh.devices.reshape(4, 4, 2, mesh.shape["head"]), ("seq_0", "seq_1", "seq_2", "head")
    )
    return jax.shard_map(
        per_device,
        mesh=torus,
        in_specs=(
            P(SEQ, None),
            P(None, "head"),
            P(None, "head"),
            P(),
            P(None, "head"),
            P(None, "head"),
            P(),
            P("head"),
            P(),
            P("head"),
            P("head"),
            P("head"),
            P("head"),
            P("head", None),
        ),
        out_specs=P(SEQ_HEAD, None),
        check_vma=False,
    )
```

profile of v0, /device:TPU:1, one launch (start us, length us, event | category | flops | bytes accessed | tf_op | source)
XLA Modules:
  0.0 221.0 jit_solution(7218201387096128753)
XLA Ops:
  6.5 1.7 copy-done
  8.3 2.2 convolution_convert_fusion.3
  10.4 0.6 slice.207
  11.1 0.1 copy-done.7
  11.2 4.7 %collective-permute-start.1 = (bf16[3,256]{1,0:T(4,128)(2,1)}, bf16[3,256]{1,0:T(4,128)(2,1)S(1)}, u32[]{:S(2)}, u32[]{:S(2)}) collective-permute-start(bf16[3,256]{1,0:T(4,128)(2,1)} %slice.207), channel_id=1, source_target_pairs={{0,4},{4,8},{8,12},{12,16},{16,20},{20,24},{24,28},{28,32},{32,36}... | collective-permute-start | bytes 4616 | tf_op jit(solution)/shard_map/ppermute | solution.py:19
  15.9 6.4 %convolution_convert_fusion.2 = bf16[512,1280]{1,0:T(8,128)(2,1)S(1)} fusion(bf16[512,2560]{1,0:T(8,128)(2,1)S(1)} %copy-done, bf16[2560,1280]{1,0:T(8,128)(2,1)} %param.15), kind=kOutput, calls=%fused_computation.5 | convolution fusion | flops 3356098560 | bytes 10485760 | tf_op jit(solution)/shard_map/dot_general | solution.py:97
  22.3 1.1 copy-done.4
  23.4 1.9 collective-permute-start
  25.3 0.0 copy-start.11
  25.4 0.8 broadcast_multiply_fusion.1
  26.2 0.1 copy.81
  26.4 0.3 reduce_window_sum.11
  26.7 0.5 exponential_reduce_fusion
  27.2 0.1 copy.72
  27.4 0.1 pad_maximum_fusion.3
  27.5 0.9 fusion.67
  28.4 0.1 slice_reduce_fusion.3
  28.5 0.1 copy.73
  28.6 1.8 multiply_convert_fusion.5
  30.4 0.7 fusion.68
  31.1 5.2 %multiply_convert_fusion.3 = bf16[512,1280]{1,0:T(8,128)(2,1)} fusion(bf16[512,1280]{1,0:T(8,128)(2,1)} %copy-done.4, bf16[3,1280]{1,0:T(4,128)(2,1)S(1)} %collective-permute-done, f32[1280]{0:T(1024)S(1)} %get-tuple-element.7, f32[1280]{0:T(1024)S(1)} %get-tuple-element.8, f32[1280]{0:T(1024)S(1)} %get-tuple-element.6, f32[1280]{0:T(1024)S(1)} %get-tuple-element.5, ...), kind=kLoop, calls=%fused_computation.24 | loop fusion | flops 17039360 | bytes 2654720 | tf_op jit(solution)/shard_map/convert_element_type | solution.py:69
  36.3 2.4 %copy.65 = bf16[512,1280]{0,1:T(8,128)(2,1)} copy(bf16[512,1280]{1,0:T(8,128)(2,1)} %multiply_convert_fusion.3) | data formatting | bytes 2621440 | tf_op jit(solution)/shard_map/convert_element_type | solution.py:69
  38.7 3.6 %reshape.130 = bf16[4,128,20,64]{1,0,3,2:T(4,128)(2,1)} reshape(bf16[512,1280]{0,1:T(8,128)(2,1)} %copy.65) | data formatting | bytes 2621440 | tf_op jit(solution)/shard_map/reshape | solution.py:111
  42.3 1.9 convert_multiply_fusion.1
  44.2 1.4 fusion.13
  45.6 1.5 slice_add_fusion.10
  47.1 0.0 all-gather.7.cloned.1.call-update
  47.1 0.0 all-gather.9.cloned.1.call-start
  47.1 1.2 dynamic-slice.1
  48.4 1.3 dynamic-slice
  50.9 0.8 dynamic-update-slice
  51.7 2.6 %all-reduce = f32[40]{0:T(128)S(1)} all-reduce(f32[40]{0:T(128)S(1)} %dynamic-update-slice), channel_id=2, replica_groups=mesh['seq_0'=4,'seq_1'=4,'seq_2'=2,'head'=4] {'seq_2'}, use_global_device_ids=true, to_apply=%add | all-reduce | flops 40 | bytes 320
  54.3 0.7 fusion.66
  54.9 8.7 %all-reduce.1 = f32[80]{0:T(128)S(1)} all-reduce(f32[80]{0:T(128)S(1)} %get-tuple-element.45), channel_id=3, replica_groups=mesh['seq_0'=4,'seq_1'=4,'seq_2'=2,'head'=4] {'seq_1'}, use_global_device_ids=true, to_apply=%add.1 | all-reduce | flops 80 | bytes 640
  63.6 0.6 multiply_bitcast_fusion.1
  64.3 2.3 %slice_add_fusion.8 = f32[1,20,128,64]{2,3,1,0:T(8,128)} fusion(f32[2,20,128,64]{2,3,1,0:T(8,128)} %all-gather.7.cloned.1.call-done, f32[20]{0:T(128)S(1)} %get-tuple-element.42, f32[20]{0:T(128)} %get-tuple-element.46), kind=kLoop, calls=%fused_computation.49 | loop fusion | flops 491520 | bytes 1966240 | tf_op jit(solution)/shard_map/add | solution.py:75
  66.6 0.0 all-gather.9.cloned.1.call-update
  66.6 0.0 all-gather.11.cloned.1.call-start
  66.7 0.6 fusion.70
  67.3 35.7 %all-gather.9.cloned.1.call-done = f32[4,20,128,64]{2,3,1,0:T(8,128)} async-done(((f32[1,20,128,64]{2,3,1,0:T(8,128)}), f32[4,20,128,64]{2,3,1,0:T(8,128)}) %all-gather.9.cloned.1.call-update) | async-done | bytes 2621456 | tf_op jit(solution)/shard_map/all_gather | solution.py:33
  103.0 2.8 %slice_add_fusion.4 = f32[1,20,128,64]{2,3,1,0:T(8,128)} fusion(f32[4,20,128,64]{2,3,1,0:T(8,128)} %all-gather.9.cloned.1.call-done, f32[20]{0:T(128)} %get-tuple-element.44, f32[20]{0:T(128)} %get-tuple-element.43, f32[20]{0:T(128)S(1)} %get-tuple-element.38, f32[20]{0:T(128)S(1)} %copy-done.13), kind=kLoop, calls=%fused_computation.45 | loop fusion | flops 1146880 | bytes 3277120 | tf_op jit(solution)/shard_map/add | solution.py:75
  105.8 0.0 all-gather.11.cloned.1.call-update
  105.8 1.4 copy.69
  107.2 0.7 copy.67
  108.0 1.1 copy.75
  109.0 1.1 copy.71
  110.1 0.7 mul.500
  110.8 0.1 mul.501
  110.9 8.2 %all-gather.2 = f32[4,1,20]{2,1,0:T(1,128)S(1)} all-gather(f32[1,1,20]{2,1,0:T(1,128)} %get-tuple-element.37), channel_id=1, replica_groups=mesh['seq_0'=4,'seq_1'=4,'seq_2'=2,'head'=4] {'seq_0'}, dimensions={0}, use_global_device_ids=true | all-gather | bytes 400 | tf_op jit(solution)/shard_map/all_gather | solution.py:33
  119.1 1.2 fusion.71
  120.3 0.1 stack_broadcast_in_dim.3
  120.4 1.5 pad_maximum_fusion
  121.9 2.8 %fusion.72 = f32[4,128,1280]{1,2,0} fusion(bf16[4,128,128]{2,1,0:T(8,128)(2,1)S(1)} %bitcast.85, f32[4,128,1280]{1,2,0:T(8,128)S(1)} %bitcast.78), kind=kOutput, calls=%fused_computation.139 | convolution fusion | flops 1006632960 | bytes 5373952
  124.8 3.6 %fusion = f32[4,20,64,128]{3,2,1,0:T(8,128)} fusion(f32[4,20,128]{2,1,0:T(8,128)S(1)} %copy-done.10, f32[4,20,128]{2,1,0:T(8,128)S(1)} %copy-done.9, f32[4,128,128]{2,1,0:T(8,128)S(1)} %fusion.71, pred[128,128]{1,0:T(8,128)(4,1)S(1)} %iota_compare_fusion, bf16[4,128,20,64]{1,0,3,2:T(4,128)(2,1)S(1)} %copy-done.2), kind=kOutput, calls=%fused_computation.6 | convolution fusion | flops 175636480 | bytes 4292608 | tf_op jit(solution)/shard_map/chij,cjhp->cihp/dot_general | solution.py:125
  128.4 13.0 %all-gather.11.cloned.1.call-done = f32[4,20,128,64]{2,3,1,0:T(8,128)} async-done(((f32[1,20,128,64]{2,3,1,0:T(8,128)}), f32[4,20,128,64]{2,3,1,0:T(8,128)}) %all-gather.11.cloned.1.call-update) | async-done | bytes 2621456 | tf_op jit(solution)/shard_map/all_gather | solution.py:33
  141.4 6.0 %bitcast_add_fusion = f32[4,128,20,64]{1,3,2,0:T(8,128)S(1)} fusion(f32[4,20,64,128]{3,2,1,0:T(8,128)} %fusion, f32[4,128,20,64]{1,3,2,0:T(8,128)} %bitcast.81, bf16[4,128,128,1]{2,1,3,0:T(8,128)(2,1)S(1)} %bitcast.86, f32[4,128,20]{1,2,0:T(8,128)S(1)} %copy.75, f32[4,128,20]{1,2,0:T(8,128)S(1)} %copy.71, ...), kind=kOutput, calls=%fused_computation.13 | convolution fusion | flops 1013678080 | bytes 14631722 | tf_op jit(solution)/shard_map/cin,hnp->cihp/dot_general | solution.py:160
  147.5 1.9 copy.76
  149.4 1.8 copy.91
  151.2 3.2 %copy.77 = f32[512,1280]{1,0:T(8,128)} copy(f32[512,1280]{0,1:T(8,128)} %bitcast.80) | data formatting | bytes 5242880 | tf_op jit(solution)/shard_map/reshape | solution.py:163
  154.4 8.7 %multiply_reduce_fusion = (f32[512]{0:T(512)S(1)}, f32[512,1280]{1,0:T(8,128)}) fusion(bf16[512,2560]{1,0:T(8,128)(2,1)S(1)} %copy-done, bf16[2560,1280]{1,0:T(8,128)(2,1)} %param.16, f32[512,1280]{1,0:T(8,128)} %copy.77, bf16[512,1280]{1,0:T(8,128)(2,1)} %multiply_convert_fusion.3, f32[1280]{0:T(1024)S(1)} %mul.501), kind=kOutput, calls=%fused_computation.17 | convolution fusion | flops 3363307008 | bytes 15735808 | tf_op jit(solution)/shard_map/dot_general | solution.py:98
  163.2 7.9 %all_to_all.11 = f32[4,1,512]{2,1,0:T(1,128)S(1)} all-to-all(f32[4,1,512]{2,1,0:T(1,128)S(1)} %broadcast_in_dim.24), channel_id=1, replica_groups=mesh['seq_0'=4,'seq_1'=4,'seq_2'=2,'head'=4] {'head'}, dimensions={0} | all-to-all | bytes 16384 | tf_op jit(solution)/shard_map/all_to_all | solution.py:45
  171.1 7.3 %convolution_convert_fusion = bf16[512,2560]{1,0:T(8,128)(2,1)S(1)} fusion(bf16[1280,2560]{1,0:T(8,128)(2,1)} %param.27, f32[512,1280]{1,0:T(8,128)} %get-tuple-element.50, f32[1280]{0:T(1024)S(1)} %copy-done.19, f32[512]{0:T(512)S(1)} %add_rsqrt_fusion), kind=kOutput, calls=%fused_computation.1 | convolution fusion | flops 3358720000 | bytes 11803648 | tf_op jit(solution)/shard_map/dot_general | solution.py:173
  178.4 32.9 %all_to_all.12 = bf16[4,128,2560]{2,1,0:T(8,128)(2,1)} all-to-all(bf16[4,128,2560]{2,1,0:T(8,128)(2,1)S(1)} %bitcast.82), channel_id=1, replica_groups=mesh['seq_0'=4,'seq_1'=4,'seq_2'=2,'head'=4] {'head'}, dimensions={0} | all-to-all | bytes 5242880 | tf_op jit(solution)/shard_map/all_to_all | solution.py:59
  211.3 3.1 %reduce_sum.32 = bf16[128,2560]{1,0:T(8,128)(2,1)} reduce(bf16[4,128,2560]{2,1,0:T(8,128)(2,1)} %all_to_all.12, bf16[]{:T(256)} %constant.50.clone.1), dimensions={0}, to_apply=%region_4.5 | reduce | flops 983040 | bytes 3276802 | tf_op jit(solution)/shard_map/reduce_sum | solution.py:60
  (56 shorter events, 0.2 us)
Async XLA Ops:
  6.5 1.7 copy-start
  6.5 57.8 %all-gather.7.cloned.1.call-start = ((), (), s32[]{:S(2)}) async-start(), calls=%async_computation.2 | async-start | bytes 1966080 | tf_op jit(solution)/shard_map/all_gather | solution.py:33
  10.4 0.7 copy-start.7
  11.1 14.2 %copy-start.20 = (f32[20]{0:T(128)S(1)}, f32[20]{0:T(128)}, u32[]{:S(2)}) copy-start(f32[20]{0:T(128)} %param.24) | copy-start | bytes 244
  11.1 14.2 %copy-start.8 = (bf16[2560,20]{0,1:T(8,128)(2,1)S(1)}, bf16[2560,20]{0,1:T(8,128)(2,1)}, u32[]{:S(2)}) copy-start(bf16[2560,20]{0,1:T(8,128)(2,1)} %param.18) | copy-start | bytes 307204
  11.1 14.2 %copy-start.18 = (f32[20]{0:T(128)S(1)}, f32[20]{0:T(128)}, u32[]{:S(2)}) copy-start(f32[20]{0:T(128)} %param.23) | copy-start | bytes 244
  11.2 17.4 %collective-permute-start.1 = (bf16[3,256]{1,0:T(4,128)(2,1)}, bf16[3,256]{1,0:T(4,128)(2,1)S(1)}, u32[]{:S(2)}, u32[]{:S(2)}) collective-permute-start(bf16[3,256]{1,0:T(4,128)(2,1)} %slice.207), channel_id=1, source_target_pairs={{0,4},{4,8},{8,12},{12,16},{16,20},{20,24},{24,28},{28,32},{32,36}... | collective-permute-start | bytes 4616 | tf_op jit(solution)/shard_map/ppermute | solution.py:19
  22.3 1.1 copy-start.4
  23.4 3.0 %copy-start.15 = (f32[4,256]{1,0:T(4,128)S(1)}, f32[4,256]{1,0:T(4,128)}, u32[]{:S(2)}) copy-start(f32[4,256]{1,0:T(4,128)} %param.20) | copy-start | bytes 12292
  23.4 7.7 %collective-permute-start = (bf16[3,1280]{1,0:T(4,128)(2,1)S(1)}, bf16[3,1280]{1,0:T(4,128)(2,1)S(1)}, u32[]{:S(2)}, u32[]{:S(2)}) collective-permute-start(bf16[3,1280]{1,0:T(4,128)(2,1)S(1)} %slice.202), channel_id=1, source_target_pairs={{0,4},{4,8},{8,12},{12,16},{16,20},{20,24},{24,28},{28,32},{32,36}... | collective-permute-start | bytes 23048 | tf_op jit(solution)/shard_map/ppermute | solution.py:19
  25.3 3.1 %copy-start.11 = (f32[4,1280]{1,0:T(4,128)S(1)}, f32[4,1280]{1,0:T(4,128)}, u32[]{:S(2)}) copy-start(f32[4,1280]{1,0:T(4,128)} %param.19) | copy-start | bytes 61444
  26.2 4.9 %copy-start.12 = (f32[1280]{0:T(1024)S(1)}, f32[1280]{0:T(1024)}, u32[]{:S(2)}) copy-start(f32[1280]{0:T(1024)} %param.21) | copy-start | bytes 15364
  26.2 1.2 copy-start.6
  31.1 13.1 %copy-start.5 = (bf16[512,128]{1,0:T(8,128)(2,1)}, bf16[512,128]{1,0:T(8,128)(2,1)S(1)}, u32[]{:S(2)}) copy-start(bf16[512,128]{1,0:T(8,128)(2,1)S(1)} %get-tuple-element.20) | copy-start | bytes 393220
  47.1 55.9 %all-gather.9.cloned.1.call-start = ((), (), s32[]{:S(2)}) async-start(), calls=%async_computation.3 | async-start | bytes 3276800 | tf_op jit(solution)/shard_map/all_gather | solution.py:33
  64.3 38.7 %copy-start.13 = (f32[20]{0:T(128)S(1)}, f32[20]{0:T(128)}, u32[]{:S(2)}) copy-start(f32[20]{0:T(128)} %get-tuple-element.39) | copy-start | bytes 244
  66.6 74.8 %all-gather.11.cloned.1.call-start = ((), (), s32[]{:S(2)}) async-start(), calls=%async_computation.4 | async-start | bytes 3276800 | tf_op jit(solution)/shard_map/all_gather | solution.py:33
  120.3 1.5 copy-start.3
  121.9 2.8 %copy-start.2 = (bf16[4,128,20,64]{1,0,3,2:T(4,128)(2,1)S(1)}, bf16[4,128,20,64]{1,0,3,2:T(4,128)(2,1)}, u32[]{:S(2)}) copy-start(bf16[4,128,20,64]{1,0,3,2:T(4,128)(2,1)} %reshape.130) | copy-start | bytes 3932164
  121.9 2.8 %copy-start.9 = (f32[4,20,128]{2,1,0:T(8,128)S(1)}, f32[4,20,128]{2,1,0:T(8,128)}, u32[]{:S(2)}) copy-start(f32[4,20,128]{2,1,0:T(8,128)} %copy.67) | copy-start | bytes 122884
  121.9 2.8 %copy-start.10 = (f32[4,20,128]{2,1,0:T(8,128)S(1)}, f32[4,20,128]{2,1,0:T(8,128)}, u32[]{:S(2)}) copy-start(f32[4,20,128]{2,1,0:T(8,128)} %copy.69) | copy-start | bytes 122884
  124.7 16.7 %copy-start.1 = (f32[1,20,128,64]{2,3,1,0:T(8,128)S(1)}, f32[1,20,128,64]{2,3,1,0:T(8,128)}, u32[]{:S(2)}) copy-start(f32[1,20,128,64]{2,3,1,0:T(8,128)} %slice_add_fusion.8) | copy-start | bytes 1966084
  124.8 16.7 %copy-start.14 = (f32[20]{0:T(128)S(1)}, f32[20]{0:T(128)}, u32[]{:S(2)}) copy-start(f32[20]{0:T(128)} %get-tuple-element.44) | copy-start | bytes 244
  124.8 16.7 %copy-start.16 = (f32[20]{0:T(128)S(1)}, f32[20]{0:T(128)}, u32[]{:S(2)}) copy-start(f32[20]{0:T(128)} %get-tuple-element.40) | copy-start | bytes 244
  124.8 16.7 %copy-start.17 = (f32[20]{0:T(128)S(1)}, f32[20]{0:T(128)}, u32[]{:S(2)}) copy-start(f32[20]{0:T(128)} %get-tuple-element.41) | copy-start | bytes 244
  154.4 16.7 %copy-start.19 = (f32[1280]{0:T(1024)S(1)}, f32[1280]{0:T(1024)}, u32[]{:S(2)}) copy-start(f32[1280]{0:T(1024)} %param.26) | copy-start | bytes 15364
Sparse Core Ops, SparseCore 0:
  47.2 14.4 all-gather.6
  66.7 36.2 all-gather.8
  106.0 35.4 all-gather.10
where the time goes:
time: 224 us; the launch traced here: 221 us
  blocking collectives  60.3 us (27%)
  waiting for transfers between devices  48.8 us (22%)
  matrix products  40.4 us (18%)
  local copies, waits for them, and re-layouts  26.8 us (12%)
  other arithmetic  23.3 us (10%)
  between operations  14.7 us (7%)
  starting transfers between devices  6.71 us (3%)
    all_gather x3, waiting for transfers between devices, carried_in(): pieces = jax.tree.map(lambda part: lax.all_gather(part, axis), running)  48.7 us
    all_to_all x1, blocking collectives, summed_on_arrival(): lax.all_to_all(pieces, axis, split_axis=0, concat_axis=0, tiled=True)  32.9 us
    unnamed x2, blocking collectives  11.3 us
    dot_general x1, matrix products, per_device(): jnp.dot(tokens, proj_gate, preferred_element_type=jnp.float32)  8.72 us
    all_gather x1, blocking collectives, carried_in(): pieces = jax.tree.map(lambda part: lax.all_gather(part, axis), running)  8.16 us
    unnamed x48, local copies, waits for them, and re-layouts  8.04 us
    all_to_all x1, blocking collectives, sent_to_all(): return lax.all_to_all(copies, axis, split_axis=0, concat_axis=0, tiled=True)  7.92 us
    dot_general x1, matrix products, per_device(): jnp.dot(gated_out, out_weight, preferred_element_type=jnp.float32)  7.28 us
  transfers between devices with their start and end apart: 5, of which 2 were waited for; matrix products, arithmetic and copies ran while one was open for 14% of the time, Pallas kernels for 0%

commit v1 on v0

v1 whole, which is shorter than its diff:
```python
import functools

import jax
import jax.numpy as jnp
from jax import lax
from jax.experimental import pallas as pl
from jax.experimental.pallas import tpu as pltpu
from jax.sharding import PartitionSpec as P

HEADDIM = 64
STATE = 128
KERNEL = 4
SPAN = 128
HALO = 16
CHUNK = 256
LOG2E = 1.4426950408889634
EPS = 0.25
MESH = pl.DeviceIdType.MESH
F32 = jnp.float32
BF16 = jnp.bfloat16
LINK = jnp.bfloat16


def silu(v):
    return v / (1.0 + jnp.exp(-v))


def dot(a, b):
    return jnp.dot(a, b, preferred_element_type=F32)


def kernel(
    seqs,
    parts,
    inner_all,
    tokens_hbm,
    wi_hbm,
    wg_hbm,
    wbc_hbm,
    wst_hbm,
    conv_i,
    conv_b,
    off_i,
    off_b,
    bias,
    decay_log,
    skip,
    norm_w,
    wo_hbm,
    out,
    tok,
    wi,
    wg,
    wbc,
    wst,
    wo,
    raw,
    xs_ref,
    bc_ref,
    wt_ref,
    cum_ref,
    dt_ref,
    gate,
    part_a,
    part_b,
    state,
    prior,
    st_send,
    st_recv,
    dec_send,
    dec_recv,
    pf_send,
    pf_recv,
    s_in,
    gw,
    far_send,
    far_recv,
    own_send,
    own_recv,
    comb_send,
    comb_recv,
    mine,
    sq_send,
    sq_recv,
    load_sem,
    halo_sem,
    dec_ss,
    dec_rs,
    st_ss,
    st_rs,
    pf_ss,
    pf_rs,
    far_ss,
    far_rs,
    own_ss,
    own_rs,
    comb_ss,
    comb_rs,
    sq_ss,
    sq_rs,
):
    r = lax.axis_index("seq")
    g = lax.axis_index("head")
    rows = tokens_hbm.shape[0]
    width = wi_hbm.shape[1]
    spans = rows // SPAN
    heads = width // HEADDIM
    pairs = heads // 2
    chunks = width // CHUNK
    half = width // 2
    right = lax.rem(g + 1, parts)
    left = lax.rem(g + parts - 1, parts)
    across = lax.rem(g + 2, parts)

    def loaded(src, dst, number):
        return pltpu.make_async_copy(src, dst, load_sem.at[number])

    tok_load = loaded(tokens_hbm, tok.at[pl.ds(HALO, rows), :], 0)
    wst_load = loaded(wst_hbm, wst, 1)
    wbc_load = loaded(wbc_hbm, wbc, 2)
    wg_load = [
        loaded(wg_hbm.at[:, pl.ds(c * CHUNK, CHUNK)], wg.at[c], 3 + c) for c in range(chunks)
    ]
    wi_load = [
        loaded(wi_hbm.at[:, pl.ds(c * CHUNK, CHUNK)], wi.at[c], 3 + chunks + c)
        for c in range(chunks)
    ]
    wo_load = [
        loaded(wo_hbm.at[:, pl.ds(c * CHUNK, CHUNK)], wo.at[c], 3 + 2 * chunks + c)
        for c in range(2 * chunks)
    ]
    tok_load.start()
    wst_load.start()
    wg_load[0].start()
    wg_load[1].start()
    wg_load[2].start()
    wbc_load.start()
    for c in range(chunks):
        wi_load[c].start()
    for c in range(3, chunks):
        wg_load[c].start()
    for c in range(2 * chunks):
        wo_load[c].start()

    barrier = pltpu.get_barrier_semaphore()

    def greet_seq(i, carry):
        pl.semaphore_signal(
            barrier,
            inc=1,
            device_id={"seq": lax.rem(r + i, seqs), "head": g},
            device_id_type=MESH,
        )
        return carry

    lax.fori_loop(1, seqs, greet_seq, 0)
    for other in (right, left, across):
        pl.semaphore_signal(
            barrier, inc=1, device_id={"seq": r, "head": other}, device_id_type=MESH
        )

    def far_copy(src, dst, ss, rs, seq, head):
        return pltpu.make_async_remote_copy(
            src_ref=src,
            dst_ref=dst,
            send_sem=ss,
            recv_sem=rs,
            device_id={"seq": seq, "head": head},
            device_id_type=MESH,
        )

    tok_load.wait()
    pl.semaphore_wait(barrier, seqs + 2)

    halo = far_copy(
        tok.at[pl.ds(rows, HALO), :],
        tok.at[pl.ds(0, HALO), :],
        halo_sem.at[0],
        halo_sem.at[1],
        lax.rem(r + 1, seqs),
        g,
    )

    @pl.when(r < seqs - 1)
    def _():
        halo.start()

    lane = lax.broadcasted_iota(jnp.int32, (SPAN, SPAN), 1)
    sub = lax.broadcasted_iota(jnp.int32, (SPAN, SPAN), 0)
    low = lane < HEADDIM
    low_row = low[:1]
    tri = jnp.where(lane <= sub, 1.0, 0.0).astype(F32)
    wst_load.wait()
    step = dot(tok[pl.ds(HALO, rows), :], wst[...]) + bias[...]
    tail = jnp.exp(-jnp.abs(step))
    up = 1.0 + tail
    log1p = jnp.where(up == 1.0, tail, jnp.log(up) * (tail / jnp.where(up == 1.0, 1.0, up - 1.0)))
    dt = jnp.maximum(step, 0.0) + log1p
    log_a = dt * (-LOG2E * jnp.exp(decay_log[...]))
    dt_ref[...] = jnp.zeros_like(dt_ref)
    part_a[:, pl.ds(0, SPAN)] = jnp.zeros((rows, SPAN), F32)
    dt_ref[:, pl.ds(0, heads)] = dt
    part_a[:, pl.ds(0, heads)] = log_a
    for k in range(spans):
        cum_ref[pl.ds(k * SPAN, SPAN), :] = jnp.dot(
            tri,
            part_a[pl.ds(k * SPAN, SPAN), pl.ds(0, SPAN)],
            preferred_element_type=F32,
            precision=lax.Precision.HIGHEST,
        )

    def gate_chunk(c):
        wg_load[c].wait()
        v = dot(tok[pl.ds(HALO, rows), :], wg[c]).astype(BF16).astype(F32)
        gate[:, pl.ds(c * CHUNK, CHUNK)] = silu(v)

    for c in range(3):
        gate_chunk(c)

    @pl.when(r == 0)
    def _():
        tok[pl.ds(0, HALO), :] = jnp.zeros((HALO, tok.shape[1]), BF16)

    @pl.when(r > 0)
    def _():
        halo.wait_recv()

    @pl.when(r < seqs - 1)
    def _():
        halo.wait_send()

    def conv(slot, taps, offset, cols):
        acc = offset[:, cols]
        for k in range(KERNEL):
            acc = acc + taps[pl.ds(k, 1), cols] * raw[slot, pl.ds(HALO - KERNEL + 1 + k, rows), :]
        return silu(acc).astype(BF16)

    def raw_chunk(slot, weights):
        raw[slot] = dot(tok[...], weights).astype(BF16).astype(F32)

    wbc_load.wait()
    raw_chunk(0, wbc[...])
    wi_load[0].wait()
    raw_chunk(1, wi[0])
    bc_ref[...] = conv(0, conv_b, off_b, pl.ds(0, 2 * STATE))
    for k in range(spans):
        wt_ref[k] = bc_ref[pl.ds(k * SPAN, SPAN), pl.ds(0, STATE)].astype(F32).T.astype(BF16)
    for c in range(1, chunks + 1):
        if c < chunks:
            wi_load[c].wait()
            raw_chunk((c + 1) % 2, wi[c])
        cols = pl.ds((c - 1) * CHUNK, CHUNK)
        xs_ref[:, cols] = conv(c % 2, conv_i, off_i, cols)

    state[...] = jnp.zeros_like(state)

    def local_state(k, carry):
        at = pl.ds(pl.multiple_of(k * SPAN, SPAN), SPAN)
        cum = cum_ref[at, :]
        last = cum[SPAN - 1 :, :]
        end_w = jnp.exp2(jnp.minimum(last - cum, 0.0)) * dt_ref[at, :]
        decay = jnp.exp2(last)
        wt = wt_ref[k]
        for p in range(pairs):
            cols = pl.ds(p * SPAN, SPAN)
            x = xs_ref[at, cols].astype(F32)
            w = jnp.where(
                low,
                jnp.broadcast_to(end_w[:, 2 * p : 2 * p + 1], (SPAN, SPAN)),
                jnp.broadcast_to(end_w[:, 2 * p + 1 : 2 * p + 2], (SPAN, SPAN)),
            )
            d = jnp.where(
                low_row,
                jnp.broadcast_to(decay[:, 2 * p : 2 * p + 1], (1, SPAN)),
                jnp.broadcast_to(decay[:, 2 * p + 1 : 2 * p + 2], (1, SPAN)),
            )
            held = state[:, cols]
            prior[k, :, cols] = held.astype(BF16)
            state[:, cols] = d * held + dot(wt, (x * w).astype(BF16))
        return carry

    lax.fori_loop(0, spans, local_state, 0)

    total = jnp.zeros((1, SPAN), F32)
    for k in range(spans):
        total = total + cum_ref[pl.ds(k * SPAN + SPAN - 1, 1), :]
    total = jnp.exp2(total)
    tiles = STATE // 8
    for p in range(pairs):
        side, at = divmod(p * SPAN, half)
        cols = pl.ds(at, SPAN)
        dec_send[side, :, cols] = jnp.where(
            low_row,
            jnp.broadcast_to(total[:, 2 * p : 2 * p + 1], (1, SPAN)),
            jnp.broadcast_to(total[:, 2 * p + 1 : 2 * p + 2], (1, SPAN)),
        )
        st_send[side, :, :, cols] = (
            state[:, pl.ds(p * SPAN, SPAN)].reshape(tiles, 8, SPAN).astype(LINK)
        )

    my_tile = r // 2
    my_side = lax.rem(r, 2)

    def dec_copy(i, src):
        peer = lax.rem(r + i, seqs)
        return far_copy(
            dec_send.at[lax.rem(peer, 2)], dec_recv.at[src], dec_ss.at[i], dec_rs.at[src], peer, g
        )

    def st_copy(i, src):
        peer = lax.rem(r + i, seqs)
        return far_copy(
            st_send.at[lax.rem(peer, 2), peer // 2],
            st_recv.at[src],
            st_ss.at[i],
            st_rs.at[src],
            peer,
            g,
        )

    def send_state(i, carry):
        dec_copy(i, r).start()
        st_copy(i, r).start()
        return carry

    lax.fori_loop(1, seqs, send_state, 0)
    dec_recv[r] = dec_send[my_side]
    st_recv[r] = st_send[my_side, my_tile]

    for c in range(3, chunks):
        gate_chunk(c)

    def within(k, carry):
        at = pl.ds(pl.multiple_of(k * SPAN, SPAN), SPAN)
        cum = cum_ref[at, :]
        cum_t = cum.T
        dt_t = dt_ref[at, :].T
        read = bc_ref[at, pl.ds(STATE, STATE)]
        write_t = wt_ref[k]
        scores = jnp.where(lane <= sub, dot(read, write_t), 0.0)
        base = carry
        for p in range(pairs):
            cols = pl.ds(p * SPAN, SPAN)
            x = xs_ref[at, cols]
            shown = []
            weights = []
            for h in (2 * p, 2 * p + 1):
                spread = jnp.broadcast_to(cum[:, h : h + 1], (SPAN, SPAN))
                shown.append(spread)
                gap = jnp.minimum(spread - cum_t[h : h + 1, :], 0.0)
                weights.append((scores * jnp.exp2(gap) * dt_t[h : h + 1, :]).astype(BF16))
            zero = jnp.zeros_like(x)
            both = jnp.concatenate([jnp.where(low, x, zero), jnp.where(low, zero, x)], axis=0)
            intra = dot(jnp.concatenate(weights, axis=1), both)
            scale = jnp.exp2(jnp.where(low, shown[0], shown[1]))
            inter = scale * dot(read, prior[k, :, cols])
            ahead = jnp.exp2(
                jnp.where(
                    low_row,
                    jnp.broadcast_to(base[:, 2 * p : 2 * p + 1], (1, SPAN)),
                    jnp.broadcast_to(base[:, 2 * p + 1 : 2 * p + 2], (1, SPAN)),
                )
            )
            gain = jnp.where(
                low_row,
                jnp.broadcast_to(skip[:, 2 * p : 2 * p + 1], (1, SPAN)),
                jnp.broadcast_to(skip[:, 2 * p + 1 : 2 * p + 2], (1, SPAN)),
            )
            opened = gate[at, cols]
            part_a[at, cols] = (intra + inter + gain * x.astype(F32)) * opened
            part_b[at, cols] = scale * ahead * opened
        return base + cum[SPAN - 1 :, :]

    lax.fori_loop(0, spans, within, jnp.zeros((1, SPAN), F32))

    def await_state(i, carry):
        src = lax.rem(r + i, seqs)
        dec_copy(i, src).wait_recv()
        st_copy(i, src).wait_recv()
        return carry

    lax.fori_loop(1, seqs, await_state, 0)

    def scan(d, carry):
        pf_send[d] = carry.astype(LINK)
        return dec_recv[d] * carry + st_recv[d].astype(F32)

    lax.fori_loop(0, seqs, scan, jnp.zeros((8, half), F32))

    def pf_copy(i, src):
        peer = lax.rem(r + i, seqs)
        return far_copy(
            pf_send.at[peer],
            pf_recv.at[lax.rem(src, 2), src // 2],
            pf_ss.at[i],
            pf_rs.at[src],
            peer,
            g,
        )

    def send_prefix(i, carry):
        pf_copy(i, r).start()
        return carry

    lax.fori_loop(1, seqs, send_prefix, 0)
    pf_recv[my_side, my_tile] = pf_send[r]

    def drain_state(i, carry):
        dec_copy(i, r).wait_send()
        st_copy(i, r).wait_send()
        return carry

    lax.fori_loop(1, seqs, drain_state, 0)
    for c in range(2 * chunks):
        wo_load[c].wait()

    def await_prefix(i, carry):
        pf_copy(i, lax.rem(r + i, seqs)).wait_recv()
        return carry

    lax.fori_loop(1, seqs, await_prefix, 0)
    for side in range(2):
        s_in[:, pl.ds(side * half, half)] = (
            pf_recv[side].astype(F32).reshape(STATE, half).astype(BF16)
        )

    eye = jnp.where(lane == sub, 1.0, 0.0).astype(F32)

    def gated(slot, block):
        at = pl.ds(pl.multiple_of(block * SPAN, SPAN), SPAN)
        read = bc_ref[at, pl.ds(STATE, STATE)]
        squares = jnp.zeros((SPAN, CHUNK), F32)
        for c in range(chunks):
            cols = pl.ds(c * CHUNK, CHUNK)
            pre = part_a[at, cols] + part_b[at, cols] * dot(read, s_in[:, cols])
            squares = squares + pre * pre
            gw[slot, :, cols] = (pre * norm_w[:, cols]).astype(BF16)
        column = jnp.sum(squares, axis=1, keepdims=True)
        row = jnp.sum(eye * column, axis=0, keepdims=True)
        sq_send[slot] = jnp.broadcast_to(row, (8, SPAN))

    def sq_copy(slot, offset):
        return far_copy(
            sq_send.at[slot],
            sq_recv.at[offset - 1],
            sq_ss.at[offset - 1],
            sq_rs.at[offset - 1],
            r,
            lax.rem(g + offset, parts),
        )

    def stream(send, recv, ss, rs, c, way):
        at = way * chunks + c
        return far_copy(
            send.at[at], recv.at[at], ss.at[at], rs.at[at], r, (right, left)[way]
        )

    def far_step(c, carry):
        for way in range(2):
            far_send[way * chunks + c] = dot(gw[0], wo[way * chunks + c]).astype(BF16)
            stream(far_send, far_recv, far_ss, far_rs, c, way).start()
        return carry

    def own_step(c, carry):
        for way in range(2):
            own_send[way * chunks + c] = dot(gw[1 + way], wo[(1 - way) * chunks + c]).astype(BF16)
            stream(own_send, own_recv, own_ss, own_rs, c, way).start()
        return carry

    def mine_step(c, carry):
        mine[c] = dot(gw[3], wo[c])
        return carry

    def comb_step(c, carry):
        for way in range(2):
            at = way * chunks + c
            value = dot(gw[1 + way], wo[at])
            stream(far_send, far_recv, far_ss, far_rs, c, way).wait_recv()
            comb_send[at] = (value + far_recv[at].astype(F32)).astype(BF16)
            stream(comb_send, comb_recv, comb_ss, comb_rs, c, way).start()
        return carry

    gated(0, across)
    sq_copy(0, 2).start()
    lax.fori_loop(0, chunks, far_step, 0)
    gated(1, right)
    sq_copy(1, 1).start()
    gated(2, left)
    sq_copy(2, 3).start()
    lax.fori_loop(0, chunks, own_step, 0)
    gated(3, g)
    lax.fori_loop(0, 2 * chunks, mine_step, 0)
    lax.fori_loop(0, chunks, comb_step, 0)

    squares = sq_send[3]
    for slot, offset in ((1, 1), (0, 2), (2, 3)):
        sq_copy(slot, offset).wait_recv()
        squares = squares + sq_recv[offset - 1]
    scale_row = 1.0 / jnp.sqrt(squares[:1] * (1.0 / inner_all) + EPS)
    scale = jnp.sum(eye * scale_row, axis=1, keepdims=True)

    for c in range(chunks):
        stream(own_send, own_recv, own_ss, own_rs, c, 1).wait_recv()
        stream(comb_send, comb_recv, comb_ss, comb_rs, c, 0).wait_recv()
        value = mine[c] + own_recv[chunks + c].astype(F32) + comb_recv[c].astype(F32)
        out[:, pl.ds(c * CHUNK, CHUNK)] = (value * scale).astype(BF16)
        stream(own_send, own_recv, own_ss, own_rs, c, 0).wait_recv()
        stream(comb_send, comb_recv, comb_ss, comb_rs, c, 1).wait_recv()
        value = mine[chunks + c] + own_recv[c].astype(F32) + comb_recv[chunks + c].astype(F32)
        out[:, pl.ds((chunks + c) * CHUNK, CHUNK)] = (value * scale).astype(BF16)

    def drain(c, carry):
        for way in range(2):
            stream(far_send, far_recv, far_ss, far_rs, c, way).wait_send()
            stream(own_send, own_recv, own_ss, own_rs, c, way).wait_send()
            stream(comb_send, comb_recv, comb_ss, comb_rs, c, way).wait_send()
        return carry

    lax.fori_loop(0, chunks, drain, 0)
    for slot, offset in ((1, 1), (0, 2), (2, 3)):
        sq_copy(slot, offset).wait_send()

    def drain_prefix(i, carry):
        pf_copy(i, r).wait_send()
        return carry

    lax.fori_loop(1, seqs, drain_prefix, 0)


def per_device(
    seqs,
    parts,
    tokens,
    proj_inner,
    proj_gate,
    proj_bc,
    proj_step,
    conv_inner,
    conv_bc,
    offset_inner,
    offset_bc,
    step_bias,
    decay_log,
    skip_gain,
    norm_weight,
    out_weight,
):
    rows, depth = tokens.shape
    width = proj_inner.shape[1]
    heads = step_bias.shape[0]
    chunks = width // CHUNK
    spans = rows // SPAN
    half = width // 2
    tiles = STATE // 8
    model = out_weight.shape[1]
    any_spec = pl.BlockSpec(memory_space=pl.ANY)
    vmem = pl.BlockSpec(memory_space=pltpu.VMEM)
    dma = pltpu.SemaphoreType.DMA
    streams = [pltpu.VMEM((2 * chunks, SPAN, CHUNK), BF16)] * 6
    scratch = [
        pltpu.VMEM((rows + HALO, depth), BF16),
        pltpu.VMEM((chunks, depth, CHUNK), BF16),
        pltpu.VMEM((chunks, depth, CHUNK), BF16),
        pltpu.VMEM((depth, 2 * STATE), BF16),
        pltpu.VMEM((depth, heads), BF16),
        pltpu.VMEM((2 * chunks, width, CHUNK), BF16),
        pltpu.VMEM((2, rows + HALO, CHUNK), F32),
        pltpu.VMEM((rows, width), BF16),
        pltpu.VMEM((rows, 2 * STATE), BF16),
        pltpu.VMEM((spans, STATE, SPAN), BF16),
        pltpu.VMEM((rows, SPAN), F32),
        pltpu.VMEM((rows, SPAN), F32),
        pltpu.VMEM((rows, width), F32),
        pltpu.VMEM((rows, width), F32),
        pltpu.VMEM((rows, width), F32),
        pltpu.VMEM((STATE, width), F32),
        pltpu.VMEM((spans, STATE, width), BF16),
        pltpu.VMEM((2, tiles, 8, half), LINK),
        pltpu.VMEM((seqs, 8, half), LINK),
        pltpu.VMEM((2, 1, half), F32),
        pltpu.VMEM((seqs, 1, half), F32),
        pltpu.VMEM((seqs, 8, half), LINK),
        pltpu.VMEM((2, tiles, 8, half), LINK),
        pltpu.VMEM((STATE, width), BF16),
        pltpu.VMEM((4, SPAN, width), BF16),
        *streams,
        pltpu.VMEM((2 * chunks, SPAN, CHUNK), F32),
        pltpu.VMEM((4, 8, SPAN), F32),
        pltpu.VMEM((3, 8, SPAN), F32),
        dma((3 + 4 * chunks,)),
        dma((2,)),
        *[dma((seqs,))] * 6,
        *[dma((2 * chunks,))] * 6,
        dma((3,)),
        dma((3,)),
    ]
    row = lambda v: v.reshape(1, -1)
    return pl.pallas_call(
        functools.partial(kernel, seqs, parts, float(parts * width)),
        out_shape=jax.ShapeDtypeStruct((rows // parts, model), BF16),
        in_specs=[any_spec] * 5 + [vmem] * 8 + [any_spec],
        out_specs=vmem,
        scratch_shapes=scratch,
        compiler_params=pltpu.CompilerParams(
            collective_id=0, has_side_effects=True, vmem_limit_bytes=62 * 1024 * 1024
        ),
    )(
        tokens,
        proj_inner,
        proj_gate,
        proj_bc,
        proj_step,
        conv_inner,
        conv_bc,
        row(offset_inner),
        row(offset_bc),
        row(step_bias),
        row(decay_log),
        row(skip_gain),
        row(norm_weight),
        out_weight,
    )


def solution(mesh):
    body = functools.partial(per_device, mesh.shape["seq"], mesh.shape["head"])
    return jax.shard_map(
        body,
        mesh=mesh,
        in_specs=(
            P("seq", None),
            P(None, "head"),
            P(None, "head"),
            P(),
            P(None, "head"),
            P(None, "head"),
            P(),
            P("head"),
            P(),
            P("head"),
            P("head"),
            P("head"),
            P("head"),
            P("head", None),
        ),
        out_specs=P(("seq", "head"), None),
        check_vma=False,
    )
```

time: 224 us -> 78.7 us (0.35); the launches traced: 221 us -> 78.3 us
  Pallas kernels: 0 us -> 71.8 us
  blocking collectives: 60.3 us -> 0 us
  waiting for transfers between devices: 48.8 us -> 0 us
  matrix products: 40.4 us -> 0 us
  other arithmetic: 23.3 us -> 0 us
  local copies, waits for them, and re-layouts: 26.8 us -> 6.56 us
  between operations: 14.7 us -> 0.01 us
  starting transfers between devices: 6.71 us -> 0 us
    pallas_call x0 -> x1, Pallas kernels: none -> 71.8 us  [per_device(): pl.pallas_call(functools.partial(kernel, seqs, parts, float(parts * width...]
    all_gather x3 -> x0, waiting for transfers between devices: 48.7 us -> none  [carried_in(): pieces = jax.tree.map(lambda part: lax.all_gather(part, axis), running)]
    all_to_all x2 -> x0, blocking collectives: 40.8 us -> none  [the longest x1 32.9 us: summed_on_arrival(): lax.all_to_all(pieces, axis, split_axis=0, concat_axis=0, tiled=True)]
    dot_general x9 -> x0, matrix products: 37.6 us -> none  [the longest x1 8.72 us: per_device(): jnp.dot(tokens, proj_gate, preferred_element_type=jnp.float32)]
    unnamed x2 -> x0, blocking collectives: 11.3 us -> none
    all_gather x1 -> x0, blocking collectives: 8.16 us -> none  [carried_in(): pieces = jax.tree.map(lambda part: lax.all_gather(part, axis), running)]
    convert_element_type x2 -> x0, other arithmetic: 6.98 us -> none  [causal(): return jax.nn.silu(summed).astype(jnp.bfloat16)]
    ppermute x2 -> x0, starting transfers between devices: 6.62 us -> none  [passed_along(): return lax.ppermute(block, axis, route)]
  transfers between devices with their start and end apart: 5 -> 0, of which waited for: 2 -> 0; matrix products, arithmetic and copies ran while one was open for 14% -> 0% of each run, Pallas kernels for 0% -> 0%
where the time goes in v1:
time: 78.7 us; the launch traced here: 78.3 us
  Pallas kernels  71.8 us (91%)
  local copies, waits for them, and re-layouts  6.56 us (8%)
    pallas_call x1, Pallas kernels, per_device(): pl.pallas_call(functools.partial(kernel, seqs, parts, float(parts * width...  71.8 us
    unnamed x2, local copies, waits for them, and re-layouts  3.99 us
    reshape x2, local copies, waits for them, and re-layouts, per_device(): row = lambda v: v.reshape(1, -1)  2.57 us

profile of v1, /device:TPU:1, one launch (start us, length us, event | category | flops | bytes accessed | tf_op | source)
XLA Modules:
  0.0 78.3 jit_solution(17833762340108961408)
XLA Ops:
  0.0 1.3 %reshape.18.off_i = f32[1,1280]{1,0:T(1,128)} reshape(f32[1280]{0:T(1024)} %param.21) | data formatting | bytes 10240 | tf_op jit(solution)/shard_map/reshape | solution.py:597
  1.3 1.3 %reshape.23.norm_w = f32[1,1280]{1,0:T(1,128)} reshape(f32[1280]{0:T(1024)} %param.26) | data formatting | bytes 10240 | tf_op jit(solution)/shard_map/reshape | solution.py:597
  2.6 2.0 %copy.15.wst_hbm = bf16[2560,20]{1,0:T(8,128)(2,1)} copy(bf16[2560,20]{0,1:T(8,128)(2,1)} %param.18) | data formatting | bytes 204800 | tf_op args[4]
  4.6 71.8 %shard_map.136 = bf16[128,2560]{1,0:T(8,128)(2,1)} custom-call(bf16[512,2560]{1,0:T(8,128)(2,1)} %tokens_hbm.1, bf16[2560,1280]{1,0:T(8,128)(2,1)} %wi_hbm.1, bf16[2560,1280]{1,0:T(8,128)(2,1)} %wg_hbm.1, bf16[2560,256]{1,0:T(8,128)(2,1)} %wbc_hbm.1, bf16[2560,20]{1,0:T(8,128)(2,1)} %copy.15.wst_hbm, f32[4,1280]{1,0:T(4,128)} %conv_i.1, f32[4,256]{1,0:T(4,128)} %conv_b.1, ...), custom_call_target="tpu_custom_call" | custom-call | tf_op jit(solution)/shard_map/pallas_call | solution.py:598
  76.4 2.0 %copy.17 = bf16[128,2560]{1,0:T(8,128)(2,1)} copy(bf16[128,2560]{1,0:T(8,128)(2,1)} %shard_map.136) | data formatting | bytes 1310720

commit v2 on v1

--- a/solution.py
+++ b/solution.py
@@ -13,6 +13,8 @@
 SPAN = 128
 HALO = 16
 CHUNK = 256
+BLOCK = 64
+WIDE = 512
 LOG2E = 1.4426950408889634
 EPS = 0.25
 MESH = pl.DeviceIdType.MESH
@@ -27,6 +29,14 @@
 
 def dot(a, b):
     return jnp.dot(a, b, preferred_element_type=F32)
+
+
+def split(v, count):
+    terms = []
+    for _ in range(count):
+        terms.append(v.astype(BF16))
+        v = v - terms[-1].astype(F32)
+    return terms
 
 
 def kernel(
@@ -38,23 +48,34 @@
     wg_hbm,
     wbc_hbm,
     wst_hbm,
+    conv_i_hbm,
+    conv_b_hbm,
+    off_i_hbm,
+    off_b_hbm,
+    bias_hbm,
+    decay_log_hbm,
+    skip_hbm,
+    norm_hbm,
+    wo_hbm,
+    out,
     conv_i,
     conv_b,
-    off_i,
+    off_1,
     off_b,
     bias,
     decay_log,
     skip,
-    norm_w,
-    wo_hbm,
-    out,
+    norm_1,
     tok,
-    wi,
+    wa,
     wg,
-    wbc,
+    wl,
     wst,
     wo,
     raw,
+    terms,
+    spread,
+    w_end,
     xs_ref,
     bc_ref,
     wt_ref,
@@ -63,7 +84,6 @@
     gate,
     part_a,
     part_b,
-    state,
     prior,
     st_send,
     st_recv,
@@ -83,6 +103,7 @@
     sq_send,
     sq_recv,
     load_sem,
+    small_sem,
     halo_sem,
     dec_ss,
     dec_rs,
@@ -115,32 +136,49 @@
     def loaded(src, dst, number):
         return pltpu.make_async_copy(src, dst, load_sem.at[number])
 
+    wides = width // WIDE
+    rest = width - wides * WIDE
     tok_load = loaded(tokens_hbm, tok.at[pl.ds(HALO, rows), :], 0)
     wst_load = loaded(wst_hbm, wst, 1)
-    wbc_load = loaded(wbc_hbm, wbc, 2)
+    wl_load = loaded(wg_hbm.at[:, pl.ds(wides * WIDE, rest)], wl, 2)
+    wbc_load = loaded(wbc_hbm, wa.at[0, :, pl.ds(0, 2 * STATE)], 3)
+    wr_load = loaded(
+        wi_hbm.at[:, pl.ds(wides * WIDE, rest)], wa.at[0, :, pl.ds(2 * STATE, rest)], 4
+    )
+    wi_load = [
+        loaded(wi_hbm.at[:, pl.ds(c * WIDE, WIDE)], wa.at[1 + c], 5 + c) for c in range(wides)
+    ]
     wg_load = [
-        loaded(wg_hbm.at[:, pl.ds(c * CHUNK, CHUNK)], wg.at[c], 3 + c) for c in range(chunks)
-    ]
-    wi_load = [
-        loaded(wi_hbm.at[:, pl.ds(c * CHUNK, CHUNK)], wi.at[c], 3 + chunks + c)
-        for c in range(chunks)
+        loaded(wg_hbm.at[:, pl.ds(c * WIDE, WIDE)], wg.at[c], 5 + wides + c) for c in range(wides)
     ]
     wo_load = [
-        loaded(wo_hbm.at[:, pl.ds(c * CHUNK, CHUNK)], wo.at[c], 3 + 2 * chunks + c)
+        loaded(wo_hbm.at[:, pl.ds(c * CHUNK, CHUNK)], wo.at[c], 5 + 2 * wides + c)
         for c in range(2 * chunks)
     ]
+    small_load = [
+        pltpu.make_async_copy(src, dst, small_sem.at[i])
+        for i, (src, dst) in enumerate(
+            (
+                (bias_hbm, bias),
+                (decay_log_hbm, decay_log),
+                (conv_b_hbm, conv_b),
+                (off_b_hbm, off_b),
+                (conv_i_hbm, conv_i),
+                (off_i_hbm, off_1),
+                (skip_hbm, skip),
+                (norm_hbm, norm_1),
+            )
+        )
+    ]
     tok_load.start()
+    for copy in small_load:
+        copy.start()
     wst_load.start()
-    wg_load[0].start()
-    wg_load[1].start()
-    wg_load[2].start()
+    wl_load.start()
     wbc_load.start()
-    for c in range(chunks):
-        wi_load[c].start()
-    for c in range(3, chunks):
-        wg_load[c].start()
-    for c in range(2 * chunks):
-        wo_load[c].start()
+    wr_load.start()
+    for copy in wi_load:
+        copy.start()
 
     barrier = pltpu.get_barrier_semaphore()
 
@@ -169,6 +207,10 @@
             device_id_type=MESH,
         )
 
+    for copy in small_load:
+        copy.wait()
+    off_i = off_1[...].reshape(1, -1)
+    norm_w = norm_1[...].reshape(1, -1)
     tok_load.wait()
     pl.semaphore_wait(barrier, seqs + 2)
 
@@ -189,33 +231,43 @@
     sub = lax.broadcasted_iota(jnp.int32, (SPAN, SPAN), 0)
     low = lane < HEADDIM
     low_row = low[:1]
-    tri = jnp.where(lane <= sub, 1.0, 0.0).astype(F32)
     wst_load.wait()
-    step = dot(tok[pl.ds(HALO, rows), :], wst[...]) + bias[...]
+    wl_load.wait()
+    own_rows = pl.ds(HALO, rows)
+    step = bias[...] + lax.dot_general(
+        tok[own_rows, :], wst[...], (((1,), (1,)), ((), ())), preferred_element_type=F32
+    )
+    gate_last = dot(tok[own_rows, :], wl[...])
     tail = jnp.exp(-jnp.abs(step))
     up = 1.0 + tail
     log1p = jnp.where(up == 1.0, tail, jnp.log(up) * (tail / jnp.where(up == 1.0, 1.0, up - 1.0)))
     dt = jnp.maximum(step, 0.0) + log1p
     log_a = dt * (-LOG2E * jnp.exp(decay_log[...]))
     dt_ref[...] = jnp.zeros_like(dt_ref)
-    part_a[:, pl.ds(0, SPAN)] = jnp.zeros((rows, SPAN), F32)
+    terms[...] = jnp.zeros_like(terms)
     dt_ref[:, pl.ds(0, heads)] = dt
-    part_a[:, pl.ds(0, heads)] = log_a
+    for t, term in enumerate(split(log_a, 3)):
+        for k in range(spans):
+            terms[pl.ds(t * SPAN, SPAN), pl.ds(k * SPAN, heads)] = term[k * SPAN : (k + 1) * SPAN]
+    tri = jnp.where(lane <= sub, 1.0, 0.0).astype(BF16)
+    cums = dot(jnp.concatenate([tri, tri, tri], axis=1), terms[...])
+    head_of = lax.broadcasted_iota(jnp.int32, (SPAN, width), 1) // HEADDIM
+    onto = jnp.where(head_of == lax.broadcasted_iota(jnp.int32, (SPAN, width), 0), 1.0, 0.0)
+    spread[pl.ds(0, SPAN), :] = onto.astype(BF16)
+    spread[pl.ds(SPAN, SPAN), :] = onto.astype(BF16)
+    ends = []
     for k in range(spans):
-        cum_ref[pl.ds(k * SPAN, SPAN), :] = jnp.dot(
-            tri,
-            part_a[pl.ds(k * SPAN, SPAN), pl.ds(0, SPAN)],
-            preferred_element_type=F32,
-            precision=lax.Precision.HIGHEST,
-        )
-
-    def gate_chunk(c):
-        wg_load[c].wait()
-        v = dot(tok[pl.ds(HALO, rows), :], wg[c]).astype(BF16).astype(F32)
-        gate[:, pl.ds(c * CHUNK, CHUNK)] = silu(v)
-
-    for c in range(3):
-        gate_chunk(c)
+        at = pl.ds(k * SPAN, SPAN)
+        cum = cums[:, k * SPAN : (k + 1) * SPAN]
+        cum_ref[at, :] = cum
+        end_w = jnp.exp2(jnp.minimum(cum[SPAN - 1 :, :] - cum, 0.0)) * dt_ref[at, :]
+        ends.append(jnp.concatenate(split(end_w, 2), axis=1))
+    w_end[...] = dot(jnp.concatenate(ends, axis=0), spread[...])
+
+    def gate_store(v, cols):
+        gate[:, cols] = silu(v.astype(BF16).astype(F32))
+
+    gate_store(gate_last, pl.ds(wides * WIDE, rest))
 
     @pl.when(r == 0)
     def _():
@@ -229,63 +281,67 @@
     def _():
         halo.wait_send()
 
-    def conv(slot, taps, offset, cols):
-        acc = offset[:, cols]
-        for k in range(KERNEL):
-            acc = acc + taps[pl.ds(k, 1), cols] * raw[slot, pl.ds(HALO - KERNEL + 1 + k, rows), :]
-        return silu(acc).astype(BF16)
-
-    def raw_chunk(slot, weights):
-        raw[slot] = dot(tok[...], weights).astype(BF16).astype(F32)
+    def raw_chunk(q):
+        v = dot(tok[...], wa[q]).astype(BF16).astype(F32)
+        for j in range(WIDE // SPAN):
+            raw[q, j] = v[:, j * SPAN : (j + 1) * SPAN]
+
+    def conv(q, j, taps, offset, col, dst):
+        cols = pl.ds(col, SPAN)
+        for b in range(rows // BLOCK):
+            acc = offset[:, cols]
+            for k in range(KERNEL):
+                at = pl.ds(HALO - KERNEL + 1 + k + b * BLOCK, BLOCK)
+                acc = acc + taps[pl.ds(k, 1), cols] * raw[q, j, at, :]
+            dst[pl.ds(b * BLOCK, BLOCK), cols] = silu(acc).astype(BF16)
+
+    tiles = STATE // 8
+
+    def local_state(col):
+        cols = pl.ds(col, SPAN)
+        p = col // SPAN
+        side, at = divmod(col, half)
+        held = jnp.zeros((STATE, SPAN), F32)
+        for k in range(spans):
+            own = pl.ds(k * SPAN, SPAN)
+            last = jnp.exp2(cum_ref[pl.ds(k * SPAN + SPAN - 1, 1), :])
+            d = jnp.where(
+                low_row,
+                jnp.broadcast_to(last[:, 2 * p : 2 * p + 1], (1, SPAN)),
+                jnp.broadcast_to(last[:, 2 * p + 1 : 2 * p + 2], (1, SPAN)),
+            )
+            prior[k, :, cols] = held.astype(BF16)
+            scaled = (xs_ref[own, cols].astype(F32) * w_end[own, cols]).astype(BF16)
+            held = d * held + dot(wt_ref[k], scaled)
+        st_send[side, :, :, pl.ds(at, SPAN)] = held.reshape(tiles, 8, SPAN).astype(LINK)
 
     wbc_load.wait()
-    raw_chunk(0, wbc[...])
+    wr_load.wait()
+    raw_chunk(0)
     wi_load[0].wait()
-    raw_chunk(1, wi[0])
-    bc_ref[...] = conv(0, conv_b, off_b, pl.ds(0, 2 * STATE))
+    for copy in wg_load:
+        copy.start()
+    raw_chunk(1)
+    for j in range(2 * STATE // SPAN):
+        conv(0, j, conv_b, off_b, j * SPAN, bc_ref)
     for k in range(spans):
         wt_ref[k] = bc_ref[pl.ds(k * SPAN, SPAN), pl.ds(0, STATE)].astype(F32).T.astype(BF16)
-    for c in range(1, chunks + 1):
-        if c < chunks:
-            wi_load[c].wait()
-            raw_chunk((c + 1) % 2, wi[c])
-        cols = pl.ds((c - 1) * CHUNK, CHUNK)
-        xs_ref[:, cols] = conv(c % 2, conv_i, off_i, cols)
-
-    state[...] = jnp.zeros_like(state)
-
-    def local_state(k, carry):
-        at = pl.ds(pl.multiple_of(k * SPAN, SPAN), SPAN)
-        cum = cum_ref[at, :]
-        last = cum[SPAN - 1 :, :]
-        end_w = jnp.exp2(jnp.minimum(last - cum, 0.0)) * dt_ref[at, :]
-        decay = jnp.exp2(last)
-        wt = wt_ref[k]
-        for p in range(pairs):
-            cols = pl.ds(p * SPAN, SPAN)
-            x = xs_ref[at, cols].astype(F32)
-            w = jnp.where(
-                low,
-                jnp.broadcast_to(end_w[:, 2 * p : 2 * p + 1], (SPAN, SPAN)),
-                jnp.broadcast_to(end_w[:, 2 * p + 1 : 2 * p + 2], (SPAN, SPAN)),
-            )
-            d = jnp.where(
-                low_row,
-                jnp.broadcast_to(decay[:, 2 * p : 2 * p + 1], (1, SPAN)),
-                jnp.broadcast_to(decay[:, 2 * p + 1 : 2 * p + 2], (1, SPAN)),
-            )
-            held = state[:, cols]
-            prior[k, :, cols] = held.astype(BF16)
-            state[:, cols] = d * held + dot(wt, (x * w).astype(BF16))
-        return carry
-
-    lax.fori_loop(0, spans, local_state, 0)
+    for j in range(rest // SPAN):
+        conv(0, 2 * STATE // SPAN + j, conv_i, off_i, wides * WIDE + j * SPAN, xs_ref)
+        local_state(wides * WIDE + j * SPAN)
+    wi_load[1].wait()
+    for copy in wo_load:
+        copy.start()
+    raw_chunk(2)
+    for q in range(wides):
+        for j in range(WIDE // SPAN):
+            conv(1 + q, j, conv_i, off_i, q * WIDE + j * SPAN, xs_ref)
+            local_state(q * WIDE + j * SPAN)
 
     total = jnp.zeros((1, SPAN), F32)
     for k in range(spans):
         total = total + cum_ref[pl.ds(k * SPAN + SPAN - 1, 1), :]
     total = jnp.exp2(total)
-    tiles = STATE // 8
     for p in range(pairs):
         side, at = divmod(p * SPAN, half)
         cols = pl.ds(at, SPAN)
@@ -294,21 +350,27 @@
             jnp.broadcast_to(total[:, 2 * p : 2 * p + 1], (1, SPAN)),
             jnp.broadcast_to(total[:, 2 * p + 1 : 2 * p + 2], (1, SPAN)),
         )
-        st_send[side, :, :, cols] = (
-            state[:, pl.ds(p * SPAN, SPAN)].reshape(tiles, 8, SPAN).astype(LINK)
-        )
 
     my_tile = r // 2
     my_side = lax.rem(r, 2)
 
+    def partner(i):
+        def turn(m):
+            return jnp.where(m == 3, 0, jnp.where(m == 2, 3, 2 - m))
+
+        slow = lax.rem(r // 8 + turn(i // 8), 4)
+        fast = lax.rem(lax.rem(r // 2, 4) + turn(lax.rem(i // 2, 4)), 4)
+        side = lax.rem(r + 1 + i, 2)
+        return (slow * 4 + fast) * 2 + side
+
     def dec_copy(i, src):
-        peer = lax.rem(r + i, seqs)
+        peer = partner(i)
         return far_copy(
             dec_send.at[lax.rem(peer, 2)], dec_recv.at[src], dec_ss.at[i], dec_rs.at[src], peer, g
         )
 
     def st_copy(i, src):
-        peer = lax.rem(r + i, seqs)
+        peer = partner(i)
         return far_copy(
             st_send.at[lax.rem(peer, 2), peer // 2],
             st_recv.at[src],
@@ -323,12 +385,13 @@
         st_copy(i, r).start()
         return carry
 
-    lax.fori_loop(1, seqs, send_state, 0)
+    lax.fori_loop(0, seqs - 1, send_state, 0)
     dec_recv[r] = dec_send[my_side]
     st_recv[r] = st_send[my_side, my_tile]
 
-    for c in range(3, chunks):
-        gate_chunk(c)
+    for c in range(wides):
+        wg_load[c].wait()
+        gate_store(dot(tok[own_rows, :], wg[c]), pl.ds(c * WIDE, WIDE))
 
     def within(k, carry):
         at = pl.ds(pl.multiple_of(k * SPAN, SPAN), SPAN)
@@ -371,15 +434,13 @@
             part_b[at, cols] = scale * ahead * opened
         return base + cum[SPAN - 1 :, :]
 
-    lax.fori_loop(0, spans, within, jnp.zeros((1, SPAN), F32))
-
     def await_state(i, carry):
-        src = lax.rem(r + i, seqs)
+        src = lax.rem(r + i + 1, seqs)
         dec_copy(i, src).wait_recv()
         st_copy(i, src).wait_recv()
         return carry
 
-    lax.fori_loop(1, seqs, await_state, 0)
+    lax.fori_loop(0, seqs - 1, await_state, 0)
 
     def scan(d, carry):
         pf_send[d] = carry.astype(LINK)
@@ -388,7 +449,7 @@
     lax.fori_loop(0, seqs, scan, jnp.zeros((8, half), F32))
 
     def pf_copy(i, src):
-        peer = lax.rem(r + i, seqs)
+        peer = partner(i)
         return far_copy(
             pf_send.at[peer],
             pf_recv.at[lax.rem(src, 2), src // 2],
@@ -402,23 +463,24 @@
         pf_copy(i, r).start()
         return carry
 
-    lax.fori_loop(1, seqs, send_prefix, 0)
+    lax.fori_loop(0, seqs - 1, send_prefix, 0)
     pf_recv[my_side, my_tile] = pf_send[r]
+    lax.fori_loop(0, spans, within, jnp.zeros((1, SPAN), F32))
 
     def drain_state(i, carry):
         dec_copy(i, r).wait_send()
         st_copy(i, r).wait_send()
         return carry
 
-    lax.fori_loop(1, seqs, drain_state, 0)
+    lax.fori_loop(0, seqs - 1, drain_state, 0)
     for c in range(2 * chunks):
         wo_load[c].wait()
 
     def await_prefix(i, carry):
-        pf_copy(i, lax.rem(r + i, seqs)).wait_recv()
-        return carry
-
-    lax.fori_loop(1, seqs, await_prefix, 0)
+        pf_copy(i, lax.rem(r + i + 1, seqs)).wait_recv()
+        return carry
+
+    lax.fori_loop(0, seqs - 1, await_prefix, 0)
     for side in range(2):
         s_in[:, pl.ds(side * half, half)] = (
             pf_recv[side].astype(F32).reshape(STATE, half).astype(BF16)
@@ -524,7 +586,7 @@
         pf_copy(i, r).wait_send()
         return carry
 
-    lax.fori_loop(1, seqs, drain_prefix, 0)
+    lax.fori_loop(0, seqs - 1, drain_prefix, 0)
 
 
 def per_device(
@@ -558,13 +620,24 @@
     dma = pltpu.SemaphoreType.DMA
     streams = [pltpu.VMEM((2 * chunks, SPAN, CHUNK), BF16)] * 6
     scratch = [
+        pltpu.VMEM((KERNEL, width), F32),
+        pltpu.VMEM((KERNEL, 2 * STATE), F32),
+        pltpu.VMEM((width,), F32),
+        pltpu.VMEM((1, 2 * STATE), F32),
+        pltpu.VMEM((1, heads), F32),
+        pltpu.VMEM((1, heads), F32),
+        pltpu.VMEM((1, heads), F32),
+        pltpu.VMEM((width,), F32),
         pltpu.VMEM((rows + HALO, depth), BF16),
-        pltpu.VMEM((chunks, depth, CHUNK), BF16),
-        pltpu.VMEM((chunks, depth, CHUNK), BF16),
-        pltpu.VMEM((depth, 2 * STATE), BF16),
-        pltpu.VMEM((depth, heads), BF16),
+        pltpu.VMEM((1 + width // WIDE, depth, WIDE), BF16),
+        pltpu.VMEM((width // WIDE, depth, WIDE), BF16),
+        pltpu.VMEM((depth, width % WIDE), BF16),
+        pltpu.VMEM((heads, depth), BF16),
         pltpu.VMEM((2 * chunks, width, CHUNK), BF16),
-        pltpu.VMEM((2, rows + HALO, CHUNK), F32),
+        pltpu.VMEM((1 + width // WIDE, WIDE // SPAN, rows + HALO, SPAN), F32),
+        pltpu.VMEM((3 * SPAN, spans * SPAN), BF16),
+        pltpu.VMEM((2 * SPAN, width), BF16),
+        pltpu.VMEM((rows, width), F32),
         pltpu.VMEM((rows, width), BF16),
         pltpu.VMEM((rows, 2 * STATE), BF16),
         pltpu.VMEM((spans, STATE, SPAN), BF16),
@@ -573,7 +646,6 @@
         pltpu.VMEM((rows, width), F32),
         pltpu.VMEM((rows, width), F32),
         pltpu.VMEM((rows, width), F32),
-        pltpu.VMEM((STATE, width), F32),
         pltpu.VMEM((spans, STATE, width), BF16),
         pltpu.VMEM((2, tiles, 8, half), LINK),
         pltpu.VMEM((seqs, 8, half), LINK),
@@ -587,7 +659,8 @@
         pltpu.VMEM((2 * chunks, SPAN, CHUNK), F32),
         pltpu.VMEM((4, 8, SPAN), F32),
         pltpu.VMEM((3, 8, SPAN), F32),
-        dma((3 + 4 * chunks,)),
+        dma((5 + 2 * (width // WIDE) + 2 * chunks,)),
+        dma((8,)),
         dma((2,)),
         *[dma((seqs,))] * 6,
         *[dma((2 * chunks,))] * 6,
@@ -597,8 +670,8 @@
     row = lambda v: v.reshape(1, -1)
     return pl.pallas_call(
         functools.partial(kernel, seqs, parts, float(parts * width)),
-        out_shape=jax.ShapeDtypeStruct((rows // parts, model), BF16),
-        in_specs=[any_spec] * 5 + [vmem] * 8 + [any_spec],
+        out_shape=pltpu.VMEM((rows // parts, model), BF16),
+        in_specs=[any_spec] * 14,
         out_specs=vmem,
         scratch_shapes=scratch,
         compiler_params=pltpu.CompilerParams(
@@ -609,15 +682,15 @@
         proj_inner,
         proj_gate,
         proj_bc,
-        proj_step,
+        proj_step.T,
         conv_inner,
         conv_bc,
-        row(offset_inner),
+        offset_inner,
         row(offset_bc),
         row(step_bias),
         row(decay_log),
         row(skip_gain),
-        row(norm_weight),
+        norm_weight,
         out_weight,
     )
 

time: 78.7 us -> 59.6 us (0.76)
  Pallas kernels: 71.8 us -> 58.7 us
  local copies, waits for them, and re-layouts: 6.56 us -> 0.84 us
    pallas_call x1, Pallas kernels: 71.8 us -> 58.7 us  [per_device(): pl.pallas_call(functools.partial(kernel, seqs, parts, float(parts * width...]
    unnamed x2 -> x1, local copies, waits for them, and re-layouts: 3.99 us -> 0.84 us
    reshape x2 -> x0, local copies, waits for them, and re-layouts: 2.57 us -> none  [per_device(): row = lambda v: v.reshape(1, -1)]
where the time goes in v2:
time: 59.6 us; the launch traced here: 59.5 us
  Pallas kernels  58.7 us (98%)
  local copies, waits for them, and re-layouts  0.84 us (1%)
    pallas_call x1, Pallas kernels, per_device(): pl.pallas_call(functools.partial(kernel, seqs, parts, float(parts * width...  58.7 us

profile of v2, /device:TPU:1, one launch (start us, length us, event | category | flops | bytes accessed | tf_op | source)
XLA Modules:
  0.0 59.5 jit_solution(10012535052289273654)
XLA Ops:
  0.0 58.7 %shard_map.136 = bf16[128,2560]{1,0:T(8,128)(2,1)S(1)} custom-call(bf16[512,2560]{1,0:T(8,128)(2,1)} %tokens_hbm.1, bf16[2560,1280]{1,0:T(8,128)(2,1)} %wi_hbm.1, bf16[2560,1280]{1,0:T(8,128)(2,1)} %wg_hbm.1, bf16[2560,256]{1,0:T(8,128)(2,1)} %wbc_hbm.1, bf16[20,2560]{1,0:T(8,128)(2,1)} %bitcast.5, f32[4,1280]{1,0:T(4,128)} %conv_i_hbm.1, ...), custom_call_target="tpu_custom_call" | custom-call | tf_op jit(solution)/shard_map/pallas_call | solution.py:671
  58.7 0.8 %copy.16 = bf16[128,2560]{1,0:T(8,128)(2,1)} copy(bf16[128,2560]{1,0:T(8,128)(2,1)S(1)} %shard_map.136) | data formatting | bytes 1310720

commit v3 on v2

--- a/solution.py
+++ b/solution.py
@@ -174,11 +174,8 @@
     for copy in small_load:
         copy.start()
     wst_load.start()
-    wl_load.start()
     wbc_load.start()
     wr_load.start()
-    for copy in wi_load:
-        copy.start()
 
     barrier = pltpu.get_barrier_semaphore()
 
@@ -212,6 +209,8 @@
     off_i = off_1[...].reshape(1, -1)
     norm_w = norm_1[...].reshape(1, -1)
     tok_load.wait()
+    for copy in wi_load:
+        copy.start()
     pl.semaphore_wait(barrier, seqs + 2)
 
     halo = far_copy(
@@ -232,12 +231,19 @@
     low = lane < HEADDIM
     low_row = low[:1]
     wst_load.wait()
-    wl_load.wait()
     own_rows = pl.ds(HALO, rows)
-    step = bias[...] + lax.dot_general(
-        tok[own_rows, :], wst[...], (((1,), (1,)), ((), ())), preferred_element_type=F32
+    step = bias[...] + jnp.concatenate(
+        [
+            lax.dot_general(
+                tok[pl.ds(HALO + side * (rows // 2), rows // 2), :],
+                wst[...],
+                (((1,), (1,)), ((), ())),
+                preferred_element_type=F32,
+            )
+            for side in range(2)
+        ],
+        axis=0,
     )
-    gate_last = dot(tok[own_rows, :], wl[...])
     tail = jnp.exp(-jnp.abs(step))
     up = 1.0 + tail
     log1p = jnp.where(up == 1.0, tail, jnp.log(up) * (tail / jnp.where(up == 1.0, 1.0, up - 1.0)))
@@ -267,7 +273,73 @@
     def gate_store(v, cols):
         gate[:, cols] = silu(v.astype(BF16).astype(F32))
 
-    gate_store(gate_last, pl.ds(wides * WIDE, rest))
+    order = [wides * WIDE + j * SPAN for j in range(rest // SPAN)]
+    order += [j * SPAN for j in range(wides * WIDE // SPAN)]
+    per_side = len(order) // 2
+    place = {col: divmod(n, per_side) for n, col in enumerate(order)}
+    my_tile = r // 2
+    my_side = lax.rem(r, 2)
+    chips = seqs // 2
+
+    def dec_copy(i, src, side, chip):
+        return far_copy(
+            dec_send.at[side],
+            dec_recv.at[src],
+            dec_ss.at[side * chips + i],
+            dec_rs.at[src],
+            chip * 2 + side,
+            g,
+        )
+
+    def st_copy(i, src, side, chip):
+        return far_copy(
+            st_send.at[side, chip],
+            st_recv.at[src],
+            st_ss.at[side * chips + i],
+            st_rs.at[src],
+            chip * 2 + side,
+            g,
+        )
+
+    def pf_copy(i, src_side, src_tile, side, chip):
+        return far_copy(
+            pf_send.at[chip * 2 + side],
+            pf_recv.at[src_side, src_tile],
+            pf_ss.at[side * chips + i],
+            pf_rs.at[src_tile * 2 + src_side],
+            chip * 2 + side,
+            g,
+        )
+
+    def chip_at(i):
+        chip = my_tile + i
+        return jnp.where(chip >= chips, chip - chips, chip)
+
+    def to_side(side, act):
+        def one(i, carry):
+            act(i, chip_at(i))
+            return carry
+
+        lax.fori_loop(1, chips, one, 0)
+
+        @pl.when(my_side != side)
+        def _():
+            act(0, my_tile)
+
+    total = jnp.zeros((1, SPAN), F32)
+    for k in range(spans):
+        total = total + cum_ref[pl.ds(k * SPAN + SPAN - 1, 1), :]
+    total = jnp.exp2(total)
+    for col, (side, n) in place.items():
+        p = col // SPAN
+        dec_send[side, :, pl.ds(n * SPAN, SPAN)] = jnp.where(
+            low_row,
+            jnp.broadcast_to(total[:, 2 * p : 2 * p + 1], (1, SPAN)),
+            jnp.broadcast_to(total[:, 2 * p + 1 : 2 * p + 2], (1, SPAN)),
+        )
+    for side in range(2):
+        to_side(side, lambda i, chip, side=side: dec_copy(i, r, side, chip).start())
+    dec_recv[r] = dec_send[my_side]
 
     @pl.when(r == 0)
     def _():
@@ -300,7 +372,7 @@
     def local_state(col):
         cols = pl.ds(col, SPAN)
         p = col // SPAN
-        side, at = divmod(col, half)
+        side, n = place[col]
         held = jnp.zeros((STATE, SPAN), F32)
         for k in range(spans):
             own = pl.ds(k * SPAN, SPAN)
@@ -313,12 +385,19 @@
             prior[k, :, cols] = held.astype(BF16)
             scaled = (xs_ref[own, cols].astype(F32) * w_end[own, cols]).astype(BF16)
             held = d * held + dot(wt_ref[k], scaled)
-        st_send[side, :, :, pl.ds(at, SPAN)] = held.reshape(tiles, 8, SPAN).astype(LINK)
+        st_send[side, :, :, pl.ds(n * SPAN, SPAN)] = held.reshape(tiles, 8, SPAN).astype(LINK)
+        if n == per_side - 1:
+            to_side(side, lambda i, chip: st_copy(i, r, side, chip).start())
+
+            @pl.when(my_side == side)
+            def _():
+                st_recv[r] = st_send[side, my_tile]
 
     wbc_load.wait()
     wr_load.wait()
     raw_chunk(0)
     wi_load[0].wait()
+    wl_load.start()
     for copy in wg_load:
         copy.start()
     raw_chunk(1)
@@ -337,61 +416,6 @@
         for j in range(WIDE // SPAN):
             conv(1 + q, j, conv_i, off_i, q * WIDE + j * SPAN, xs_ref)
             local_state(q * WIDE + j * SPAN)
-
-    total = jnp.zeros((1, SPAN), F32)
-    for k in range(spans):
-        total = total + cum_ref[pl.ds(k * SPAN + SPAN - 1, 1), :]
-    total = jnp.exp2(total)
-    for p in range(pairs):
-        side, at = divmod(p * SPAN, half)
-        cols = pl.ds(at, SPAN)
-        dec_send[side, :, cols] = jnp.where(
-            low_row,
-            jnp.broadcast_to(total[:, 2 * p : 2 * p + 1], (1, SPAN)),
-            jnp.broadcast_to(total[:, 2 * p + 1 : 2 * p + 2], (1, SPAN)),
-        )
-
-    my_tile = r // 2
-    my_side = lax.rem(r, 2)
-
-    def partner(i):
-        def turn(m):
-            return jnp.where(m == 3, 0, jnp.where(m == 2, 3, 2 - m))
-
-        slow = lax.rem(r // 8 + turn(i // 8), 4)
-        fast = lax.rem(lax.rem(r // 2, 4) + turn(lax.rem(i // 2, 4)), 4)
-        side = lax.rem(r + 1 + i, 2)
-        return (slow * 4 + fast) * 2 + side
-
-    def dec_copy(i, src):
-        peer = partner(i)
-        return far_copy(
-            dec_send.at[lax.rem(peer, 2)], dec_recv.at[src], dec_ss.at[i], dec_rs.at[src], peer, g
-        )
-
-    def st_copy(i, src):
-        peer = partner(i)
-        return far_copy(
-            st_send.at[lax.rem(peer, 2), peer // 2],
-            st_recv.at[src],
-            st_ss.at[i],
-            st_rs.at[src],
-            peer,
-            g,
-        )
-
-    def send_state(i, carry):
-        dec_copy(i, r).start()
-        st_copy(i, r).start()
-        return carry
-
-    lax.fori_loop(0, seqs - 1, send_state, 0)
-    dec_recv[r] = dec_send[my_side]
-    st_recv[r] = st_send[my_side, my_tile]
-
-    for c in range(wides):
-        wg_load[c].wait()
-        gate_store(dot(tok[own_rows, :], wg[c]), pl.ds(c * WIDE, WIDE))
 
     def within(k, carry):
         at = pl.ds(pl.multiple_of(k * SPAN, SPAN), SPAN)
@@ -434,57 +458,72 @@
             part_b[at, cols] = scale * ahead * opened
         return base + cum[SPAN - 1 :, :]
 
-    def await_state(i, carry):
-        src = lax.rem(r + i + 1, seqs)
-        dec_copy(i, src).wait_recv()
-        st_copy(i, src).wait_recv()
-        return carry
-
-    lax.fori_loop(0, seqs - 1, await_state, 0)
-
-    def scan(d, carry):
-        pf_send[d] = carry.astype(LINK)
-        return dec_recv[d] * carry + st_recv[d].astype(F32)
-
-    lax.fori_loop(0, seqs, scan, jnp.zeros((8, half), F32))
-
-    def pf_copy(i, src):
-        peer = partner(i)
-        return far_copy(
-            pf_send.at[peer],
-            pf_recv.at[lax.rem(src, 2), src // 2],
-            pf_ss.at[i],
-            pf_rs.at[src],
-            peer,
-            g,
-        )
-
-    def send_prefix(i, carry):
-        pf_copy(i, r).start()
-        return carry
-
-    lax.fori_loop(0, seqs - 1, send_prefix, 0)
-    pf_recv[my_side, my_tile] = pf_send[r]
+    def own_scan(side):
+        @pl.when(my_side == side)
+        def _():
+            def arrived(src):
+                far = far_copy(
+                    st_send.at[side, 0], st_recv.at[src], st_ss.at[0], st_rs.at[src], r, g
+                )
+                near = far_copy(
+                    dec_send.at[side], dec_recv.at[src], dec_ss.at[0], dec_rs.at[src], r, g
+                )
+                far.wait_recv()
+                near.wait_recv()
+
+            def await_state(i, carry):
+                chip = chip_at(i)
+                arrived(chip * 2)
+                arrived(chip * 2 + 1)
+                return carry
+
+            lax.fori_loop(1, chips, await_state, 0)
+            arrived(my_tile * 2 + (1 - side))
+
+            def scan(d, carry):
+                pf_send[d] = carry.astype(LINK)
+                return dec_recv[d] * carry + st_recv[d].astype(F32)
+
+            lax.fori_loop(0, seqs, scan, jnp.zeros((8, half), F32))
+            for other in range(2):
+                to_side(
+                    other,
+                    lambda i, chip, other=other: pf_copy(i, side, my_tile, other, chip).start(),
+                )
+            pf_recv[side, my_tile] = pf_send[r]
+
+    def gate_wide(c):
+        wg_load[c].wait()
+        gate_store(dot(tok[own_rows, :], wg[c]), pl.ds(c * WIDE, WIDE))
+
+    gate_wide(0)
+    wl_load.wait()
+    gate_store(dot(tok[own_rows, :], wl[...]), pl.ds(wides * WIDE, rest))
+    own_scan(0)
+    gate_wide(1)
+    own_scan(1)
     lax.fori_loop(0, spans, within, jnp.zeros((1, SPAN), F32))
-
-    def drain_state(i, carry):
-        dec_copy(i, r).wait_send()
-        st_copy(i, r).wait_send()
-        return carry
-
-    lax.fori_loop(0, seqs - 1, drain_state, 0)
     for c in range(2 * chunks):
         wo_load[c].wait()
 
-    def await_prefix(i, carry):
-        pf_copy(i, lax.rem(r + i + 1, seqs)).wait_recv()
-        return carry
-
-    lax.fori_loop(0, seqs - 1, await_prefix, 0)
-    for side in range(2):
-        s_in[:, pl.ds(side * half, half)] = (
-            pf_recv[side].astype(F32).reshape(STATE, half).astype(BF16)
-        )
+    def prefix_from(side):
+        def await_prefix(i, carry):
+            pf_copy(i, side, chip_at(i), 0, 0).wait_recv()
+            return carry
+
+        lax.fori_loop(1, chips, await_prefix, 0)
+
+        @pl.when(my_side != side)
+        def _():
+            pf_copy(0, side, my_tile, 0, 0).wait_recv()
+
+        got = pf_recv[side].astype(F32).reshape(STATE, half).astype(BF16)
+        for col, (at, n) in place.items():
+            if at == side:
+                s_in[:, pl.ds(col, SPAN)] = got[:, n * SPAN : (n + 1) * SPAN]
+
+    prefix_from(0)
+    prefix_from(1)
 
     eye = jnp.where(lane == sub, 1.0, 0.0).astype(F32)
 
@@ -554,6 +593,29 @@
     lax.fori_loop(0, 2 * chunks, mine_step, 0)
     lax.fori_loop(0, chunks, comb_step, 0)
 
+    def drain(c, carry):
+        for way in range(2):
+            stream(far_send, far_recv, far_ss, far_rs, c, way).wait_send()
+            stream(own_send, own_recv, own_ss, own_rs, c, way).wait_send()
+        return carry
+
+    def drain_comb(c, carry):
+        for way in range(2):
+            stream(comb_send, comb_recv, comb_ss, comb_rs, c, way).wait_send()
+        return carry
+
+    for side in range(2):
+
+        def sent(i, chip, side=side):
+            dec_copy(i, r, side, chip).wait_send()
+            st_copy(i, r, side, chip).wait_send()
+            pf_copy(i, 0, 0, side, chip).wait_send()
+
+        to_side(side, sent)
+    for slot, offset in ((1, 1), (0, 2), (2, 3)):
+        sq_copy(slot, offset).wait_send()
+    lax.fori_loop(0, chunks, drain, 0)
+
     squares = sq_send[3]
     for slot, offset in ((1, 1), (0, 2), (2, 3)):
         sq_copy(slot, offset).wait_recv()
@@ -571,22 +633,7 @@
         value = mine[chunks + c] + own_recv[c].astype(F32) + comb_recv[chunks + c].astype(F32)
         out[:, pl.ds((chunks + c) * CHUNK, CHUNK)] = (value * scale).astype(BF16)
 
-    def drain(c, carry):
-        for way in range(2):
-            stream(far_send, far_recv, far_ss, far_rs, c, way).wait_send()
-            stream(own_send, own_recv, own_ss, own_rs, c, way).wait_send()
-            stream(comb_send, comb_recv, comb_ss, comb_rs, c, way).wait_send()
-        return carry
-
-    lax.fori_loop(0, chunks, drain, 0)
-    for slot, offset in ((1, 1), (0, 2), (2, 3)):
-        sq_copy(slot, offset).wait_send()
-
-    def drain_prefix(i, carry):
-        pf_copy(i, r).wait_send()
-        return carry
-
-    lax.fori_loop(0, seqs - 1, drain_prefix, 0)
+    lax.fori_loop(0, chunks, drain_comb, 0)
 
 
 def per_device(

time: 59.6 us -> 58.6 us (0.983)
  Pallas kernels: 58.7 us -> 57.7 us
    pallas_call x1, Pallas kernels: 58.7 us -> 57.7 us  [per_device(): pl.pallas_call(functools.partial(kernel, seqs, parts, float(parts * width...]
where the time goes in v3:
time: 58.6 us; the launch traced here: 58.5 us
  Pallas kernels  57.7 us (98%)
  local copies, waits for them, and re-layouts  0.84 us (1%)
    pallas_call x1, Pallas kernels, per_device(): pl.pallas_call(functools.partial(kernel, seqs, parts, float(parts * width...  57.7 us

profile of v3, /device:TPU:1, one launch (start us, length us, event | category | flops | bytes accessed | tf_op | source)
XLA Modules:
  0.0 58.5 jit_solution(247628056496360059)
XLA Ops:
  0.0 57.7 %shard_map.136 = bf16[128,2560]{1,0:T(8,128)(2,1)S(1)} custom-call(bf16[512,2560]{1,0:T(8,128)(2,1)} %tokens_hbm.1, bf16[2560,1280]{1,0:T(8,128)(2,1)} %wi_hbm.1, bf16[2560,1280]{1,0:T(8,128)(2,1)} %wg_hbm.1, bf16[2560,256]{1,0:T(8,128)(2,1)} %wbc_hbm.1, bf16[20,2560]{1,0:T(8,128)(2,1)} %bitcast.5, f32[4,1280]{1,0:T(4,128)} %conv_i_hbm.1, ...), custom_call_target="tpu_custom_call" | custom-call | tf_op jit(solution)/shard_map/pallas_call | solution.py:718
  57.7 0.8 %copy.16 = bf16[128,2560]{1,0:T(8,128)(2,1)} copy(bf16[128,2560]{1,0:T(8,128)(2,1)S(1)} %shard_map.136) | data formatting | bytes 1310720

commit v4 on v3

--- a/solution.py
+++ b/solution.py
@@ -11,7 +11,7 @@
 STATE = 128
 KERNEL = 4
 SPAN = 128
-HALO = 16
+HALO = 8
 CHUNK = 256
 BLOCK = 64
 WIDE = 512
@@ -92,6 +92,7 @@
     pf_send,
     pf_recv,
     s_in,
+    held_scan,
     gw,
     far_send,
     far_recv,
@@ -138,7 +139,7 @@
 
     wides = width // WIDE
     rest = width - wides * WIDE
-    tok_load = loaded(tokens_hbm, tok.at[pl.ds(HALO, rows), :], 0)
+    tok_load = loaded(tokens_hbm, tok, 0)
     wst_load = loaded(wst_hbm, wst, 1)
     wl_load = loaded(wg_hbm.at[:, pl.ds(wides * WIDE, rest)], wl, 2)
     wbc_load = loaded(wbc_hbm, wa.at[0, :, pl.ds(0, 2 * STATE)], 3)
@@ -204,63 +205,79 @@
             device_id_type=MESH,
         )
 
+    lane = lax.broadcasted_iota(jnp.int32, (SPAN, SPAN), 1)
+    sub = lax.broadcasted_iota(jnp.int32, (SPAN, SPAN), 0)
+    low = lane < HEADDIM
+    low_row = low[:1]
+    head_of = lax.broadcasted_iota(jnp.int32, (SPAN, width), 1) // HEADDIM
+    onto = jnp.where(head_of == lax.broadcasted_iota(jnp.int32, (SPAN, width), 0), 1.0, 0.0)
+    spread[pl.ds(0, SPAN), :] = onto.astype(BF16)
+    spread[pl.ds(SPAN, SPAN), :] = onto.astype(BF16)
+    terms[...] = jnp.zeros_like(terms)
+    dt_ref[...] = jnp.zeros_like(dt_ref)
+    wst_load.wait()
+    tok_load.wait()
+    for copy in wi_load:
+        copy.start()
+    for side in range(2):
+        at = pl.ds(side * (rows // 2), rows // 2)
+        dt_ref[at, pl.ds(0, heads)] = lax.dot_general(
+            tok[at, :], wst[...], (((1,), (1,)), ((), ())), preferred_element_type=F32
+        )
+
+    def raw_chunk(q):
+        v = dot(tok[...], wa[q]).astype(BF16).astype(F32)
+        for j in range(WIDE // SPAN):
+            raw[q, j, pl.ds(HALO, rows), :] = v[:, j * SPAN : (j + 1) * SPAN]
+
+    wbc_load.wait()
+    wr_load.wait()
+    raw_chunk(0)
+    for q in range(wides):
+        wi_load[q].wait()
+        raw_chunk(1 + q)
+    wl_load.start()
+    for copy in wg_load:
+        copy.start()
+    for copy in wo_load:
+        copy.start()
+
+    pl.semaphore_wait(barrier, seqs + 2)
+
+    edges = [
+        far_copy(
+            raw.at[q, :, pl.ds(rows, HALO), :],
+            raw.at[q, :, pl.ds(0, HALO), :],
+            halo_sem.at[q],
+            halo_sem.at[1 + wides + q],
+            lax.rem(r + 1, seqs),
+            g,
+        )
+        for q in range(1 + wides)
+    ]
+
+    @pl.when(r < seqs - 1)
+    def _():
+        for edge in edges:
+            edge.start()
+
     for copy in small_load:
         copy.wait()
     off_i = off_1[...].reshape(1, -1)
     norm_w = norm_1[...].reshape(1, -1)
-    tok_load.wait()
-    for copy in wi_load:
-        copy.start()
-    pl.semaphore_wait(barrier, seqs + 2)
-
-    halo = far_copy(
-        tok.at[pl.ds(rows, HALO), :],
-        tok.at[pl.ds(0, HALO), :],
-        halo_sem.at[0],
-        halo_sem.at[1],
-        lax.rem(r + 1, seqs),
-        g,
-    )
-
-    @pl.when(r < seqs - 1)
-    def _():
-        halo.start()
-
-    lane = lax.broadcasted_iota(jnp.int32, (SPAN, SPAN), 1)
-    sub = lax.broadcasted_iota(jnp.int32, (SPAN, SPAN), 0)
-    low = lane < HEADDIM
-    low_row = low[:1]
-    wst_load.wait()
-    own_rows = pl.ds(HALO, rows)
-    step = bias[...] + jnp.concatenate(
-        [
-            lax.dot_general(
-                tok[pl.ds(HALO + side * (rows // 2), rows // 2), :],
-                wst[...],
-                (((1,), (1,)), ((), ())),
-                preferred_element_type=F32,
-            )
-            for side in range(2)
-        ],
-        axis=0,
-    )
+
+    step = dt_ref[:, pl.ds(0, heads)] + bias[...]
     tail = jnp.exp(-jnp.abs(step))
     up = 1.0 + tail
     log1p = jnp.where(up == 1.0, tail, jnp.log(up) * (tail / jnp.where(up == 1.0, 1.0, up - 1.0)))
     dt = jnp.maximum(step, 0.0) + log1p
     log_a = dt * (-LOG2E * jnp.exp(decay_log[...]))
-    dt_ref[...] = jnp.zeros_like(dt_ref)
-    terms[...] = jnp.zeros_like(terms)
     dt_ref[:, pl.ds(0, heads)] = dt
     for t, term in enumerate(split(log_a, 3)):
         for k in range(spans):
             terms[pl.ds(t * SPAN, SPAN), pl.ds(k * SPAN, heads)] = term[k * SPAN : (k + 1) * SPAN]
     tri = jnp.where(lane <= sub, 1.0, 0.0).astype(BF16)
     cums = dot(jnp.concatenate([tri, tri, tri], axis=1), terms[...])
-    head_of = lax.broadcasted_iota(jnp.int32, (SPAN, width), 1) // HEADDIM
-    onto = jnp.where(head_of == lax.broadcasted_iota(jnp.int32, (SPAN, width), 0), 1.0, 0.0)
-    spread[pl.ds(0, SPAN), :] = onto.astype(BF16)
-    spread[pl.ds(SPAN, SPAN), :] = onto.astype(BF16)
     ends = []
     for k in range(spans):
         at = pl.ds(k * SPAN, SPAN)
@@ -281,50 +298,43 @@
     my_side = lax.rem(r, 2)
     chips = seqs // 2
 
-    def dec_copy(i, src, side, chip):
+    def dec_copy(dst):
         return far_copy(
-            dec_send.at[side],
-            dec_recv.at[src],
-            dec_ss.at[side * chips + i],
-            dec_rs.at[src],
-            chip * 2 + side,
-            g,
-        )
-
-    def st_copy(i, src, side, chip):
+            dec_send.at[lax.rem(dst, 2)], dec_recv.at[r], dec_ss.at[dst], dec_rs.at[r], dst, g
+        )
+
+    def st_copy(side, chip):
+        dst = chip * 2 + side
         return far_copy(
-            st_send.at[side, chip],
-            st_recv.at[src],
-            st_ss.at[side * chips + i],
-            st_rs.at[src],
-            chip * 2 + side,
-            g,
-        )
-
-    def pf_copy(i, src_side, src_tile, side, chip):
+            st_send.at[side, chip], st_recv.at[r], st_ss.at[dst], st_rs.at[r], dst, g
+        )
+
+    def pf_copy(dst):
         return far_copy(
-            pf_send.at[chip * 2 + side],
-            pf_recv.at[src_side, src_tile],
-            pf_ss.at[side * chips + i],
-            pf_rs.at[src_tile * 2 + src_side],
-            chip * 2 + side,
-            g,
-        )
-
-    def chip_at(i):
-        chip = my_tile + i
-        return jnp.where(chip >= chips, chip - chips, chip)
+            pf_send.at[dst], pf_recv.at[my_side, my_tile], pf_ss.at[dst], pf_rs.at[r], dst, g
+        )
+
+    def each(first, last, act):
+        def one(d, carry):
+            @pl.when(d != r)
+            def _():
+                act(d)
+
+            return carry
+
+        lax.fori_loop(first, last, one, 0)
 
     def to_side(side, act):
         def one(i, carry):
-            act(i, chip_at(i))
+            chip = my_tile + i
+            act(side, jnp.where(chip >= chips, chip - chips, chip))
             return carry
 
         lax.fori_loop(1, chips, one, 0)
 
         @pl.when(my_side != side)
         def _():
-            act(0, my_tile)
+            act(side, my_tile)
 
     total = jnp.zeros((1, SPAN), F32)
     for k in range(spans):
@@ -337,26 +347,17 @@
             jnp.broadcast_to(total[:, 2 * p : 2 * p + 1], (1, SPAN)),
             jnp.broadcast_to(total[:, 2 * p + 1 : 2 * p + 2], (1, SPAN)),
         )
-    for side in range(2):
-        to_side(side, lambda i, chip, side=side: dec_copy(i, r, side, chip).start())
+    each(0, seqs, lambda d: dec_copy(d).start())
     dec_recv[r] = dec_send[my_side]
 
     @pl.when(r == 0)
     def _():
-        tok[pl.ds(0, HALO), :] = jnp.zeros((HALO, tok.shape[1]), BF16)
+        raw[:, :, pl.ds(0, HALO), :] = jnp.zeros((1 + wides, WIDE // SPAN, HALO, SPAN), F32)
 
     @pl.when(r > 0)
     def _():
-        halo.wait_recv()
-
-    @pl.when(r < seqs - 1)
-    def _():
-        halo.wait_send()
-
-    def raw_chunk(q):
-        v = dot(tok[...], wa[q]).astype(BF16).astype(F32)
-        for j in range(WIDE // SPAN):
-            raw[q, j] = v[:, j * SPAN : (j + 1) * SPAN]
+        for edge in edges:
+            edge.wait_recv()
 
     def conv(q, j, taps, offset, col, dst):
         cols = pl.ds(col, SPAN)
@@ -387,20 +388,12 @@
             held = d * held + dot(wt_ref[k], scaled)
         st_send[side, :, :, pl.ds(n * SPAN, SPAN)] = held.reshape(tiles, 8, SPAN).astype(LINK)
         if n == per_side - 1:
-            to_side(side, lambda i, chip: st_copy(i, r, side, chip).start())
+            to_side(side, lambda at, chip: st_copy(at, chip).start())
 
             @pl.when(my_side == side)
             def _():
                 st_recv[r] = st_send[side, my_tile]
 
-    wbc_load.wait()
-    wr_load.wait()
-    raw_chunk(0)
-    wi_load[0].wait()
-    wl_load.start()
-    for copy in wg_load:
-        copy.start()
-    raw_chunk(1)
     for j in range(2 * STATE // SPAN):
         conv(0, j, conv_b, off_b, j * SPAN, bc_ref)
     for k in range(spans):
@@ -408,10 +401,6 @@
     for j in range(rest // SPAN):
         conv(0, 2 * STATE // SPAN + j, conv_i, off_i, wides * WIDE + j * SPAN, xs_ref)
         local_state(wides * WIDE + j * SPAN)
-    wi_load[1].wait()
-    for copy in wo_load:
-        copy.start()
-    raw_chunk(2)
     for q in range(wides):
         for j in range(WIDE // SPAN):
             conv(1 + q, j, conv_i, off_i, q * WIDE + j * SPAN, xs_ref)
@@ -458,72 +447,77 @@
             part_b[at, cols] = scale * ahead * opened
         return base + cum[SPAN - 1 :, :]
 
-    def own_scan(side):
-        @pl.when(my_side == side)
+    def own_scan(first, last):
+        def arrived(src):
+            far_copy(
+                dec_send.at[my_side], dec_recv.at[src], dec_ss.at[src], dec_rs.at[src], src, g
+            ).wait_recv()
+            far_copy(
+                st_send.at[my_side, 0], st_recv.at[src], st_ss.at[src], st_rs.at[src], src, g
+            ).wait_recv()
+
+        each(first, last, arrived)
+
+        def scan(d, carry):
+            pf_send[d] = carry.astype(LINK)
+            return dec_recv[d] * carry + st_recv[d].astype(F32)
+
+        start = jnp.zeros((8, half), F32) if first == 0 else held_scan[...]
+        held_scan[...] = lax.fori_loop(first, last, scan, start)
+        each(first, last, lambda d: pf_copy(d).start())
+
+        @pl.when((r >= first) & (r < last))
         def _():
-            def arrived(src):
-                far = far_copy(
-                    st_send.at[side, 0], st_recv.at[src], st_ss.at[0], st_rs.at[src], r, g
-                )
-                near = far_copy(
-                    dec_send.at[side], dec_recv.at[src], dec_ss.at[0], dec_rs.at[src], r, g
-                )
-                far.wait_recv()
-                near.wait_recv()
-
-            def await_state(i, carry):
-                chip = chip_at(i)
-                arrived(chip * 2)
-                arrived(chip * 2 + 1)
-                return carry
-
-            lax.fori_loop(1, chips, await_state, 0)
-            arrived(my_tile * 2 + (1 - side))
-
-            def scan(d, carry):
-                pf_send[d] = carry.astype(LINK)
-                return dec_recv[d] * carry + st_recv[d].astype(F32)
-
-            lax.fori_loop(0, seqs, scan, jnp.zeros((8, half), F32))
-            for other in range(2):
-                to_side(
-                    other,
-                    lambda i, chip, other=other: pf_copy(i, side, my_tile, other, chip).start(),
-                )
-            pf_recv[side, my_tile] = pf_send[r]
+            pf_recv[my_side, my_tile] = pf_send[r]
 
     def gate_wide(c):
         wg_load[c].wait()
-        gate_store(dot(tok[own_rows, :], wg[c]), pl.ds(c * WIDE, WIDE))
-
+        gate_store(dot(tok[...], wg[c]), pl.ds(c * WIDE, WIDE))
+
+    late = r >= seqs // 2
+
+    @pl.when(late)
+    def _():
+        own_scan(0, seqs // 2)
+
+    wl_load.wait()
+    gate_store(dot(tok[...], wl[...]), pl.ds(wides * WIDE, rest))
     gate_wide(0)
-    wl_load.wait()
-    gate_store(dot(tok[own_rows, :], wl[...]), pl.ds(wides * WIDE, rest))
-    own_scan(0)
     gate_wide(1)
-    own_scan(1)
+
+    @pl.when(late)
+    def _():
+        own_scan(seqs // 2, seqs)
+
+    @pl.when(jnp.logical_not(late))
+    def _():
+        own_scan(0, seqs // 2)
+
     lax.fori_loop(0, spans, within, jnp.zeros((1, SPAN), F32))
+
+    @pl.when(jnp.logical_not(late))
+    def _():
+        own_scan(seqs // 2, seqs)
+
     for c in range(2 * chunks):
         wo_load[c].wait()
 
-    def prefix_from(side):
-        def await_prefix(i, carry):
-            pf_copy(i, side, chip_at(i), 0, 0).wait_recv()
-            return carry
-
-        lax.fori_loop(1, chips, await_prefix, 0)
-
-        @pl.when(my_side != side)
-        def _():
-            pf_copy(0, side, my_tile, 0, 0).wait_recv()
-
+    def prefix_arrived(src):
+        far_copy(
+            pf_send.at[0],
+            pf_recv.at[lax.rem(src, 2), src // 2],
+            pf_ss.at[src],
+            pf_rs.at[src],
+            src,
+            g,
+        ).wait_recv()
+
+    each(0, seqs, prefix_arrived)
+    for side in range(2):
         got = pf_recv[side].astype(F32).reshape(STATE, half).astype(BF16)
         for col, (at, n) in place.items():
             if at == side:
                 s_in[:, pl.ds(col, SPAN)] = got[:, n * SPAN : (n + 1) * SPAN]
-
-    prefix_from(0)
-    prefix_from(1)
 
     eye = jnp.where(lane == sub, 1.0, 0.0).astype(F32)
 
@@ -604,14 +598,18 @@
             stream(comb_send, comb_recv, comb_ss, comb_rs, c, way).wait_send()
         return carry
 
-    for side in range(2):
-
-        def sent(i, chip, side=side):
-            dec_copy(i, r, side, chip).wait_send()
-            st_copy(i, r, side, chip).wait_send()
-            pf_copy(i, 0, 0, side, chip).wait_send()
-
-        to_side(side, sent)
+    def sent(d):
+        dec_copy(d).wait_send()
+        st_copy(lax.rem(d, 2), d // 2).wait_send()
+        pf_copy(d).wait_send()
+
+    each(0, seqs, sent)
+
+    @pl.when(r < seqs - 1)
+    def _():
+        for edge in edges:
+            edge.wait_send()
+
     for slot, offset in ((1, 1), (0, 2), (2, 3)):
         sq_copy(slot, offset).wait_send()
     lax.fori_loop(0, chunks, drain, 0)
@@ -675,7 +673,7 @@
         pltpu.VMEM((1, heads), F32),
         pltpu.VMEM((1, heads), F32),
         pltpu.VMEM((width,), F32),
-        pltpu.VMEM((rows + HALO, depth), BF16),
+        pltpu.VMEM((rows, depth), BF16),
         pltpu.VMEM((1 + width // WIDE, depth, WIDE), BF16),
         pltpu.VMEM((width // WIDE, depth, WIDE), BF16),
         pltpu.VMEM((depth, width % WIDE), BF16),
@@ -701,6 +699,7 @@
         pltpu.VMEM((seqs, 8, half), LINK),
         pltpu.VMEM((2, tiles, 8, half), LINK),
         pltpu.VMEM((STATE, width), BF16),
+        pltpu.VMEM((8, half), F32),
         pltpu.VMEM((4, SPAN, width), BF16),
         *streams,
         pltpu.VMEM((2 * chunks, SPAN, CHUNK), F32),
@@ -708,7 +707,7 @@
         pltpu.VMEM((3, 8, SPAN), F32),
         dma((5 + 2 * (width // WIDE) + 2 * chunks,)),
         dma((8,)),
-        dma((2,)),
+        dma((2 + 2 * (width // WIDE),)),
         *[dma((seqs,))] * 6,
         *[dma((2 * chunks,))] * 6,
         dma((3,)),

time: 58.6 us -> 57.1 us (0.974)
  the two profiles are of different devices: /device:TPU:1 before, /device:TPU:64 now
where the time goes in v4:
time: 57.1 us; the launch traced here: 57 us
  Pallas kernels  56.2 us (98%)
  local copies, waits for them, and re-layouts  0.84 us (1%)
    pallas_call x1, Pallas kernels, per_device(): pl.pallas_call(functools.partial(kernel, seqs, parts, float(parts * width...  56.2 us

profile of v4, /device:TPU:64, one launch (start us, length us, event | category | flops | bytes accessed | tf_op | source)
XLA Modules:
  0.0 57.0 jit_solution(16711510203222846318)
XLA Ops:
  0.0 56.2 %shard_map.136 = bf16[128,2560]{1,0:T(8,128)(2,1)S(1)} custom-call(bf16[512,2560]{1,0:T(8,128)(2,1)} %tokens_hbm.1, bf16[2560,1280]{1,0:T(8,128)(2,1)} %wi_hbm.1, bf16[2560,1280]{1,0:T(8,128)(2,1)} %wg_hbm.1, bf16[2560,256]{1,0:T(8,128)(2,1)} %wbc_hbm.1, bf16[20,2560]{1,0:T(8,128)(2,1)} %bitcast.5, f32[4,1280]{1,0:T(4,128)} %conv_i_hbm.1, ...), custom_call_target="tpu_custom_call" | custom-call | tf_op jit(solution)/shard_map/pallas_call | solution.py:717
  56.2 0.8 %copy.16 = bf16[128,2560]{1,0:T(8,128)(2,1)} copy(bf16[128,2560]{1,0:T(8,128)(2,1)S(1)} %shard_map.136) | data formatting | bytes 1310720

commit v5 on v4

--- a/solution.py
+++ b/solution.py
@@ -15,6 +15,7 @@
 CHUNK = 256
 BLOCK = 64
 WIDE = 512
+PIECES = 4
 LOG2E = 1.4426950408889634
 EPS = 0.25
 MESH = pl.DeviceIdType.MESH
@@ -134,13 +135,30 @@
     left = lax.rem(g + parts - 1, parts)
     across = lax.rem(g + 2, parts)
 
-    def loaded(src, dst, number):
-        return pltpu.make_async_copy(src, dst, load_sem.at[number])
+    class loaded:
+        def __init__(self, src, dst, number):
+            self.whole = pltpu.make_async_copy(src, dst, load_sem.at[number])
+            block = src.shape[0] // PIECES
+            self.pieces = [
+                pltpu.make_async_copy(
+                    src.at[pl.ds(i * block, block), :],
+                    dst.at[pl.ds(i * block, block), :],
+                    load_sem.at[number],
+                )
+                for i in range(PIECES)
+            ]
+
+        def start(self):
+            for piece in self.pieces:
+                piece.start()
+
+        def wait(self):
+            self.whole.wait()
 
     wides = width // WIDE
     rest = width - wides * WIDE
     tok_load = loaded(tokens_hbm, tok, 0)
-    wst_load = loaded(wst_hbm, wst, 1)
+    wst_load = pltpu.make_async_copy(wst_hbm, wst, load_sem.at[1])
     wl_load = loaded(wg_hbm.at[:, pl.ds(wides * WIDE, rest)], wl, 2)
     wbc_load = loaded(wbc_hbm, wa.at[0, :, pl.ds(0, 2 * STATE)], 3)
     wr_load = loaded(
@@ -242,25 +260,6 @@
     for copy in wo_load:
         copy.start()
 
-    pl.semaphore_wait(barrier, seqs + 2)
-
-    edges = [
-        far_copy(
-            raw.at[q, :, pl.ds(rows, HALO), :],
-            raw.at[q, :, pl.ds(0, HALO), :],
-            halo_sem.at[q],
-            halo_sem.at[1 + wides + q],
-            lax.rem(r + 1, seqs),
-            g,
-        )
-        for q in range(1 + wides)
-    ]
-
-    @pl.when(r < seqs - 1)
-    def _():
-        for edge in edges:
-            edge.start()
-
     for copy in small_load:
         copy.wait()
     off_i = off_1[...].reshape(1, -1)
@@ -287,6 +286,25 @@
         ends.append(jnp.concatenate(split(end_w, 2), axis=1))
     w_end[...] = dot(jnp.concatenate(ends, axis=0), spread[...])
 
+    pl.semaphore_wait(barrier, seqs + 2)
+
+    edges = [
+        far_copy(
+            raw.at[q, :, pl.ds(rows, HALO), :],
+            raw.at[q, :, pl.ds(0, HALO), :],
+            halo_sem.at[q],
+            halo_sem.at[1 + wides + q],
+            lax.rem(r + 1, seqs),
+            g,
+        )
+        for q in range(1 + wides)
+    ]
+
+    @pl.when(r < seqs - 1)
+    def _():
+        for edge in edges:
+            edge.start()
+
     def gate_store(v, cols):
         gate[:, cols] = silu(v.astype(BF16).astype(F32))
 
@@ -316,13 +334,11 @@
 
     def each(first, last, act):
         def one(d, carry):
-            @pl.when(d != r)
-            def _():
-                act(d)
-
+            act(d)
             return carry
 
-        lax.fori_loop(first, last, one, 0)
+        lax.fori_loop(first, jnp.minimum(r, last), one, 0)
+        lax.fori_loop(jnp.maximum(r + 1, first), last, one, 0)
 
     def to_side(side, act):
         def one(i, carry):
@@ -350,18 +366,9 @@
     each(0, seqs, lambda d: dec_copy(d).start())
     dec_recv[r] = dec_send[my_side]
 
-    @pl.when(r == 0)
-    def _():
-        raw[:, :, pl.ds(0, HALO), :] = jnp.zeros((1 + wides, WIDE // SPAN, HALO, SPAN), F32)
-
-    @pl.when(r > 0)
-    def _():
-        for edge in edges:
-            edge.wait_recv()
-
-    def conv(q, j, taps, offset, col, dst):
+    def conv(q, j, taps, offset, col, dst, blocks):
         cols = pl.ds(col, SPAN)
-        for b in range(rows // BLOCK):
+        for b in blocks:
             acc = offset[:, cols]
             for k in range(KERNEL):
                 at = pl.ds(HALO - KERNEL + 1 + k + b * BLOCK, BLOCK)
@@ -394,17 +401,40 @@
             def _():
                 st_recv[r] = st_send[side, my_tile]
 
-    for j in range(2 * STATE // SPAN):
-        conv(0, j, conv_b, off_b, j * SPAN, bc_ref)
+    def gate_wide(c):
+        wg_load[c].wait()
+        gate_store(dot(tok[...], wg[c]), pl.ds(c * WIDE, WIDE))
+
+    main = range(1, rows // BLOCK)
+    convs = [(0, j, conv_b, off_b, j * SPAN, bc_ref) for j in range(2 * STATE // SPAN)]
+    for n, col in enumerate(order):
+        q, j = divmod(2 * STATE // SPAN + n, WIDE // SPAN)
+        convs.append((q, j, conv_i, off_i, col, xs_ref))
+    for args in convs:
+        conv(*args, main)
+
+    group = seqs // 4
+    edge_late = (lax.rem(r, group) == 0) & (r > 0)
+
+    @pl.when(edge_late)
+    def _():
+        gate_wide(0)
+
+    @pl.when(r == 0)
+    def _():
+        raw[:, :, pl.ds(0, HALO), :] = jnp.zeros((1 + wides, WIDE // SPAN, HALO, SPAN), F32)
+
+    @pl.when(r > 0)
+    def _():
+        for edge in edges:
+            edge.wait_recv()
+
+    for args in convs:
+        conv(*args, range(1))
     for k in range(spans):
         wt_ref[k] = bc_ref[pl.ds(k * SPAN, SPAN), pl.ds(0, STATE)].astype(F32).T.astype(BF16)
-    for j in range(rest // SPAN):
-        conv(0, 2 * STATE // SPAN + j, conv_i, off_i, wides * WIDE + j * SPAN, xs_ref)
-        local_state(wides * WIDE + j * SPAN)
-    for q in range(wides):
-        for j in range(WIDE // SPAN):
-            conv(1 + q, j, conv_i, off_i, q * WIDE + j * SPAN, xs_ref)
-            local_state(q * WIDE + j * SPAN)
+    for col in order:
+        local_state(col)
 
     def within(k, carry):
         at = pl.ds(pl.multiple_of(k * SPAN, SPAN), SPAN)
@@ -462,43 +492,43 @@
             pf_send[d] = carry.astype(LINK)
             return dec_recv[d] * carry + st_recv[d].astype(F32)
 
-        start = jnp.zeros((8, half), F32) if first == 0 else held_scan[...]
-        held_scan[...] = lax.fori_loop(first, last, scan, start)
+        held_scan[...] = lax.fori_loop(first, last, scan, held_scan[...])
         each(first, last, lambda d: pf_copy(d).start())
 
         @pl.when((r >= first) & (r < last))
         def _():
             pf_recv[my_side, my_tile] = pf_send[r]
 
-    def gate_wide(c):
-        wg_load[c].wait()
-        gate_store(dot(tok[...], wg[c]), pl.ds(c * WIDE, WIDE))
-
-    late = r >= seqs // 2
-
-    @pl.when(late)
+    row = r // group
+
+    def rounds(before, after):
+        def of(done):
+            return group * jnp.where(
+                row == 0,
+                done[0],
+                jnp.where(row == 1, done[1], jnp.where(row == 2, done[2], done[3])),
+            )
+
+        own_scan(of(before), of(after))
+
+    done = ((0, 0, 0, 0), (0, 0, 1, 1), (0, 1, 2, 2), (1, 2, 3, 4), (2, 4, 4, 4), (4, 4, 4, 4))
+
+    held_scan[...] = jnp.zeros((8, half), F32)
+
+    @pl.when(jnp.logical_not(edge_late))
     def _():
-        own_scan(0, seqs // 2)
-
+        gate_wide(0)
+
+    rounds(done[0], done[1])
+    gate_wide(1)
+    rounds(done[1], done[2])
     wl_load.wait()
     gate_store(dot(tok[...], wl[...]), pl.ds(wides * WIDE, rest))
-    gate_wide(0)
-    gate_wide(1)
-
-    @pl.when(late)
-    def _():
-        own_scan(seqs // 2, seqs)
-
-    @pl.when(jnp.logical_not(late))
-    def _():
-        own_scan(0, seqs // 2)
-
-    lax.fori_loop(0, spans, within, jnp.zeros((1, SPAN), F32))
-
-    @pl.when(jnp.logical_not(late))
-    def _():
-        own_scan(seqs // 2, seqs)
-
+    rounds(done[2], done[3])
+    base = lax.fori_loop(0, spans // 2, within, jnp.zeros((1, SPAN), F32))
+    rounds(done[3], done[4])
+    lax.fori_loop(spans // 2, spans, within, base)
+    rounds(done[4], done[5])
     for c in range(2 * chunks):
         wo_load[c].wait()
 

time: 57.1 us -> 54.6 us (0.956)
  the two profiles are of different devices: /device:TPU:64 before, /device:TPU:1 now
where the time goes in v5:
time: 54.6 us; the launch traced here: 54 us
  Pallas kernels  53.1 us (97%)
  local copies, waits for them, and re-layouts  0.84 us (2%)
    pallas_call x1, Pallas kernels, per_device(): pl.pallas_call(functools.partial(kernel, seqs, parts, float(parts * width...  53.1 us

profile of v5, /device:TPU:1, one launch (start us, length us, event | category | flops | bytes accessed | tf_op | source)
XLA Modules:
  0.0 54.0 jit_solution(1865492730888751231)
XLA Ops:
  0.0 53.1 %shard_map.136 = bf16[128,2560]{1,0:T(8,128)(2,1)S(1)} custom-call(bf16[512,2560]{1,0:T(8,128)(2,1)} %tokens_hbm.1, bf16[2560,1280]{1,0:T(8,128)(2,1)} %wi_hbm.1, bf16[2560,1280]{1,0:T(8,128)(2,1)} %wg_hbm.1, bf16[2560,256]{1,0:T(8,128)(2,1)} %wbc_hbm.1, bf16[20,2560]{1,0:T(8,128)(2,1)} %bitcast.5, f32[4,1280]{1,0:T(4,128)} %conv_i_hbm.1, ...), custom_call_target="tpu_custom_call" | custom-call | tf_op jit(solution)/shard_map/pallas_call | solution.py:747
  53.1 0.8 %copy.16 = bf16[128,2560]{1,0:T(8,128)(2,1)} copy(bf16[128,2560]{1,0:T(8,128)(2,1)S(1)} %shard_map.136) | data formatting | bytes 1310720

commit v6 on v5

--- a/solution.py
+++ b/solution.py
@@ -171,7 +171,9 @@
         loaded(wg_hbm.at[:, pl.ds(c * WIDE, WIDE)], wg.at[c], 5 + wides + c) for c in range(wides)
     ]
     wo_load = [
-        loaded(wo_hbm.at[:, pl.ds(c * CHUNK, CHUNK)], wo.at[c], 5 + 2 * wides + c)
+        pltpu.make_async_copy(
+            wo_hbm.at[:, pl.ds(c * CHUNK, CHUNK)], wo.at[c], load_sem.at[5 + 2 * wides]
+        )
         for c in range(2 * chunks)
     ]
     small_load = [
@@ -316,21 +318,31 @@
     my_side = lax.rem(r, 2)
     chips = seqs // 2
 
+    group = seqs // 4
+    row = r // group
+
     def dec_copy(dst):
         return far_copy(
-            dec_send.at[lax.rem(dst, 2)], dec_recv.at[r], dec_ss.at[dst], dec_rs.at[r], dst, g
+            dec_send.at[lax.rem(dst, 2)], dec_recv.at[r], dec_ss.at[0], dec_rs.at[row], dst, g
         )
 
     def st_copy(side, chip):
-        dst = chip * 2 + side
         return far_copy(
-            st_send.at[side, chip], st_recv.at[r], st_ss.at[dst], st_rs.at[r], dst, g
+            st_send.at[side, chip],
+            st_recv.at[r],
+            st_ss.at[0],
+            st_rs.at[row],
+            chip * 2 + side,
+            g,
         )
 
     def pf_copy(dst):
         return far_copy(
-            pf_send.at[dst], pf_recv.at[my_side, my_tile], pf_ss.at[dst], pf_rs.at[r], dst, g
-        )
+            pf_send.at[dst], pf_recv.at[my_side, my_tile], pf_ss.at[0], pf_rs.at[0], dst, g
+        )
+
+    def bulk(ref, ss, rs):
+        return far_copy(ref, ref, ss, rs, r, g)
 
     def each(first, last, act):
         def one(d, carry):
@@ -413,7 +425,6 @@
     for args in convs:
         conv(*args, main)
 
-    group = seqs // 4
     edge_late = (lax.rem(r, group) == 0) & (r > 0)
 
     @pl.when(edge_late)
@@ -477,16 +488,25 @@
             part_b[at, cols] = scale * ahead * opened
         return base + cum[SPAN - 1 :, :]
 
-    def own_scan(first, last):
-        def arrived(src):
-            far_copy(
-                dec_send.at[my_side], dec_recv.at[src], dec_ss.at[src], dec_rs.at[src], src, g
-            ).wait_recv()
-            far_copy(
-                st_send.at[my_side, 0], st_recv.at[src], st_ss.at[src], st_rs.at[src], src, g
-            ).wait_recv()
-
-        each(first, last, arrived)
+    def own_scan(begin, end):
+        def arrived(q, count):
+            at = pl.ds(q * group, count)
+            bulk(dec_recv.at[at], dec_ss.at[0], dec_rs.at[q]).wait_recv()
+            bulk(st_recv.at[at], st_ss.at[0], st_rs.at[q]).wait_recv()
+
+        def await_group(q, carry):
+            @pl.when(q == row)
+            def _():
+                arrived(q, group - 1)
+
+            @pl.when(q != row)
+            def _():
+                arrived(q, group)
+
+            return carry
+
+        lax.fori_loop(begin, end, await_group, 0)
+        first, last = begin * group, end * group
 
         def scan(d, carry):
             pf_send[d] = carry.astype(LINK)
@@ -499,11 +519,9 @@
         def _():
             pf_recv[my_side, my_tile] = pf_send[r]
 
-    row = r // group
-
     def rounds(before, after):
         def of(done):
-            return group * jnp.where(
+            return jnp.where(
                 row == 0,
                 done[0],
                 jnp.where(row == 1, done[1], jnp.where(row == 2, done[2], done[3])),
@@ -529,20 +547,9 @@
     rounds(done[3], done[4])
     lax.fori_loop(spans // 2, spans, within, base)
     rounds(done[4], done[5])
-    for c in range(2 * chunks):
-        wo_load[c].wait()
-
-    def prefix_arrived(src):
-        far_copy(
-            pf_send.at[0],
-            pf_recv.at[lax.rem(src, 2), src // 2],
-            pf_ss.at[src],
-            pf_rs.at[src],
-            src,
-            g,
-        ).wait_recv()
-
-    each(0, seqs, prefix_arrived)
+    pltpu.make_async_copy(wo, wo, load_sem.at[5 + 2 * wides]).wait()
+
+    bulk(pf_send.at[pl.ds(0, seqs - 1)], pf_ss.at[0], pf_rs.at[0]).wait_recv()
     for side in range(2):
         got = pf_recv[side].astype(F32).reshape(STATE, half).astype(BF16)
         for col, (at, n) in place.items():
@@ -568,8 +575,8 @@
         return far_copy(
             sq_send.at[slot],
             sq_recv.at[offset - 1],
-            sq_ss.at[offset - 1],
-            sq_rs.at[offset - 1],
+            sq_ss.at[0],
+            sq_rs.at[0],
             r,
             lax.rem(g + offset, parts),
         )
@@ -577,7 +584,12 @@
     def stream(send, recv, ss, rs, c, way):
         at = way * chunks + c
         return far_copy(
-            send.at[at], recv.at[at], ss.at[at], rs.at[at], r, (right, left)[way]
+            send.at[at],
+            recv.at[at],
+            ss.at[0],
+            rs.at[0] if rs is own_rs else rs.at[at],
+            r,
+            (right, left)[way],
         )
 
     def far_step(c, carry):
@@ -617,51 +629,35 @@
     lax.fori_loop(0, 2 * chunks, mine_step, 0)
     lax.fori_loop(0, chunks, comb_step, 0)
 
-    def drain(c, carry):
-        for way in range(2):
-            stream(far_send, far_recv, far_ss, far_rs, c, way).wait_send()
-            stream(own_send, own_recv, own_ss, own_rs, c, way).wait_send()
-        return carry
-
-    def drain_comb(c, carry):
-        for way in range(2):
-            stream(comb_send, comb_recv, comb_ss, comb_rs, c, way).wait_send()
-        return carry
-
-    def sent(d):
-        dec_copy(d).wait_send()
-        st_copy(lax.rem(d, 2), d // 2).wait_send()
-        pf_copy(d).wait_send()
-
-    each(0, seqs, sent)
+    others = pl.ds(0, seqs - 1)
+    bulk(dec_recv.at[others], dec_ss.at[0], dec_rs.at[0]).wait_send()
+    bulk(st_recv.at[others], st_ss.at[0], st_rs.at[0]).wait_send()
+    bulk(pf_send.at[others], pf_ss.at[0], pf_rs.at[0]).wait_send()
 
     @pl.when(r < seqs - 1)
     def _():
         for edge in edges:
             edge.wait_send()
 
-    for slot, offset in ((1, 1), (0, 2), (2, 3)):
-        sq_copy(slot, offset).wait_send()
-    lax.fori_loop(0, chunks, drain, 0)
-
-    squares = sq_send[3]
-    for slot, offset in ((1, 1), (0, 2), (2, 3)):
-        sq_copy(slot, offset).wait_recv()
-        squares = squares + sq_recv[offset - 1]
+    bulk(sq_recv, sq_ss.at[0], sq_rs.at[0]).wait_send()
+    bulk(far_send, far_ss.at[0], far_rs.at[0]).wait_send()
+    bulk(own_send, own_ss.at[0], own_rs.at[0]).wait_send()
+
+    bulk(sq_recv, sq_ss.at[0], sq_rs.at[0]).wait_recv()
+    squares = sq_send[3] + sq_recv[0] + sq_recv[1] + sq_recv[2]
     scale_row = 1.0 / jnp.sqrt(squares[:1] * (1.0 / inner_all) + EPS)
     scale = jnp.sum(eye * scale_row, axis=1, keepdims=True)
 
+    bulk(own_recv, own_ss.at[0], own_rs.at[0]).wait_recv()
     for c in range(chunks):
-        stream(own_send, own_recv, own_ss, own_rs, c, 1).wait_recv()
         stream(comb_send, comb_recv, comb_ss, comb_rs, c, 0).wait_recv()
         value = mine[c] + own_recv[chunks + c].astype(F32) + comb_recv[c].astype(F32)
         out[:, pl.ds(c * CHUNK, CHUNK)] = (value * scale).astype(BF16)
-        stream(own_send, own_recv, own_ss, own_rs, c, 0).wait_recv()
         stream(comb_send, comb_recv, comb_ss, comb_rs, c, 1).wait_recv()
         value = mine[chunks + c] + own_recv[c].astype(F32) + comb_recv[chunks + c].astype(F32)
         out[:, pl.ds((chunks + c) * CHUNK, CHUNK)] = (value * scale).astype(BF16)
 
-    lax.fori_loop(0, chunks, drain_comb, 0)
+    bulk(comb_send, comb_ss.at[0], comb_rs.at[0]).wait_send()
 
 
 def per_device(
@@ -735,13 +731,23 @@
         pltpu.VMEM((2 * chunks, SPAN, CHUNK), F32),
         pltpu.VMEM((4, 8, SPAN), F32),
         pltpu.VMEM((3, 8, SPAN), F32),
-        dma((5 + 2 * (width // WIDE) + 2 * chunks,)),
+        dma((6 + 2 * (width // WIDE),)),
         dma((8,)),
         dma((2 + 2 * (width // WIDE),)),
-        *[dma((seqs,))] * 6,
-        *[dma((2 * chunks,))] * 6,
-        dma((3,)),
-        dma((3,)),
+        dma((1,)),
+        dma((4,)),
+        dma((1,)),
+        dma((4,)),
+        dma((1,)),
+        dma((1,)),
+        dma((1,)),
+        dma((2 * chunks,)),
+        dma((1,)),
+        dma((1,)),
+        dma((1,)),
+        dma((2 * chunks,)),
+        dma((1,)),
+        dma((1,)),
     ]
     row = lambda v: v.reshape(1, -1)
     return pl.pallas_call(

time: 54.6 us -> 52.3 us (0.958)
  Pallas kernels: 53.1 us -> 51 us
    pallas_call x1, Pallas kernels: 53.1 us -> 51 us  [per_device(): pl.pallas_call(functools.partial(kernel, seqs, parts, float(parts * width...]
where the time goes in v6:
time: 52.3 us; the launch traced here: 51.9 us
  Pallas kernels  51 us (98%)
  local copies, waits for them, and re-layouts  0.84 us (2%)
    pallas_call x1, Pallas kernels, per_device(): pl.pallas_call(functools.partial(kernel, seqs, parts, float(parts * width...  51 us

profile of v6, /device:TPU:1, one launch (start us, length us, event | category | flops | bytes accessed | tf_op | source)
XLA Modules:
  0.0 51.9 jit_solution(2310097902294166397)
XLA Ops:
  0.0 51.0 %shard_map.136 = bf16[128,2560]{1,0:T(8,128)(2,1)S(1)} custom-call(bf16[512,2560]{1,0:T(8,128)(2,1)} %tokens_hbm.1, bf16[2560,1280]{1,0:T(8,128)(2,1)} %wi_hbm.1, bf16[2560,1280]{1,0:T(8,128)(2,1)} %wg_hbm.1, bf16[2560,256]{1,0:T(8,128)(2,1)} %wbc_hbm.1, bf16[20,2560]{1,0:T(8,128)(2,1)} %bitcast.5, f32[4,1280]{1,0:T(4,128)} %conv_i_hbm.1, ...), custom_call_target="tpu_custom_call" | custom-call | tf_op jit(solution)/shard_map/pallas_call | solution.py:753
  51.0 0.8 %copy.16 = bf16[128,2560]{1,0:T(8,128)(2,1)} copy(bf16[128,2560]{1,0:T(8,128)(2,1)S(1)} %shard_map.136) | data formatting | bytes 1310720

commit v7 on v6

--- a/solution.py
+++ b/solution.py
@@ -191,9 +191,9 @@
             )
         )
     ]
-    tok_load.start()
     for copy in small_load:
         copy.start()
+    tok_load.start()
     wst_load.start()
     wbc_load.start()
     wr_load.start()
@@ -245,28 +245,19 @@
             tok[at, :], wst[...], (((1,), (1,)), ((), ())), preferred_element_type=F32
         )
 
-    def raw_chunk(q):
-        v = dot(tok[...], wa[q]).astype(BF16).astype(F32)
+    def raw_part(q, m):
+        at = rows // 2 * m
+        v = dot(tok[pl.ds(at, rows // 2), :], wa[q]).astype(BF16).astype(F32)
         for j in range(WIDE // SPAN):
-            raw[q, j, pl.ds(HALO, rows), :] = v[:, j * SPAN : (j + 1) * SPAN]
+            raw[q, j, pl.ds(HALO + at, rows // 2), :] = v[:, j * SPAN : (j + 1) * SPAN]
 
     wbc_load.wait()
     wr_load.wait()
-    raw_chunk(0)
-    for q in range(wides):
-        wi_load[q].wait()
-        raw_chunk(1 + q)
-    wl_load.start()
-    for copy in wg_load:
-        copy.start()
-    for copy in wo_load:
-        copy.start()
-
+    raw_part(0, 1)
     for copy in small_load:
         copy.wait()
     off_i = off_1[...].reshape(1, -1)
     norm_w = norm_1[...].reshape(1, -1)
-
     step = dt_ref[:, pl.ds(0, heads)] + bias[...]
     tail = jnp.exp(-jnp.abs(step))
     up = 1.0 + tail
@@ -278,6 +269,8 @@
         for k in range(spans):
             terms[pl.ds(t * SPAN, SPAN), pl.ds(k * SPAN, heads)] = term[k * SPAN : (k + 1) * SPAN]
     tri = jnp.where(lane <= sub, 1.0, 0.0).astype(BF16)
+    wi_load[0].wait()
+    raw_part(1, 1)
     cums = dot(jnp.concatenate([tri, tri, tri], axis=1), terms[...])
     ends = []
     for k in range(spans):
@@ -288,24 +281,29 @@
         ends.append(jnp.concatenate(split(end_w, 2), axis=1))
     w_end[...] = dot(jnp.concatenate(ends, axis=0), spread[...])
 
+    for q in range(1, wides):
+        wi_load[q].wait()
+        raw_part(1 + q, 1)
+    wl_load.start()
+    for copy in wg_load:
+        copy.start()
+    for copy in wo_load:
+        copy.start()
+
     pl.semaphore_wait(barrier, seqs + 2)
 
-    edges = [
-        far_copy(
-            raw.at[q, :, pl.ds(rows, HALO), :],
-            raw.at[q, :, pl.ds(0, HALO), :],
-            halo_sem.at[q],
-            halo_sem.at[1 + wides + q],
-            lax.rem(r + 1, seqs),
-            g,
-        )
-        for q in range(1 + wides)
-    ]
+    edge = far_copy(
+        raw.at[:, :, pl.ds(rows, HALO), :],
+        raw.at[:, :, pl.ds(0, HALO), :],
+        halo_sem.at[0],
+        halo_sem.at[1],
+        lax.rem(r + 1, seqs),
+        g,
+    )
 
     @pl.when(r < seqs - 1)
     def _():
-        for edge in edges:
-            edge.start()
+        edge.start()
 
     def gate_store(v, cols):
         gate[:, cols] = silu(v.astype(BF16).astype(F32))
@@ -417,19 +415,23 @@
         wg_load[c].wait()
         gate_store(dot(tok[...], wg[c]), pl.ds(c * WIDE, WIDE))
 
-    main = range(1, rows // BLOCK)
     convs = [(0, j, conv_b, off_b, j * SPAN, bc_ref) for j in range(2 * STATE // SPAN)]
     for n, col in enumerate(order):
         q, j = divmod(2 * STATE // SPAN + n, WIDE // SPAN)
         convs.append((q, j, conv_i, off_i, col, xs_ref))
+    middle = rows // BLOCK // 2
+    upper = range(middle + 1, rows // BLOCK)
+    lower = range(1, middle + 1)
+    per_part = WIDE // SPAN
+    raw_part(0, 0)
     for args in convs:
-        conv(*args, main)
-
-    edge_late = (lax.rem(r, group) == 0) & (r > 0)
-
-    @pl.when(edge_late)
-    def _():
-        gate_wide(0)
+        conv(*args, upper)
+    for q in range(1, 1 + wides):
+        raw_part(q, 0)
+        for args in convs[(q - 1) * per_part : q * per_part]:
+            conv(*args, lower)
+    for args in convs[wides * per_part :]:
+        conv(*args, lower)
 
     @pl.when(r == 0)
     def _():
@@ -437,8 +439,7 @@
 
     @pl.when(r > 0)
     def _():
-        for edge in edges:
-            edge.wait_recv()
+        edge.wait_recv()
 
     for args in convs:
         conv(*args, range(1))
@@ -494,7 +495,11 @@
             bulk(dec_recv.at[at], dec_ss.at[0], dec_rs.at[q]).wait_recv()
             bulk(st_recv.at[at], st_ss.at[0], st_rs.at[q]).wait_recv()
 
-        def await_group(q, carry):
+        def scan(d, carry):
+            pf_send[d] = carry.astype(LINK)
+            return dec_recv[d] * carry + st_recv[d].astype(F32)
+
+        def one_group(q, carry):
             @pl.when(q == row)
             def _():
                 arrived(q, group - 1)
@@ -503,21 +508,17 @@
             def _():
                 arrived(q, group)
 
+            first, last = q * group, (q + 1) * group
+            held_scan[...] = lax.fori_loop(first, last, scan, held_scan[...])
+            each(first, last, lambda d: pf_copy(d).start())
+
+            @pl.when(q == row)
+            def _():
+                pf_recv[my_side, my_tile] = pf_send[r]
+
             return carry
 
-        lax.fori_loop(begin, end, await_group, 0)
-        first, last = begin * group, end * group
-
-        def scan(d, carry):
-            pf_send[d] = carry.astype(LINK)
-            return dec_recv[d] * carry + st_recv[d].astype(F32)
-
-        held_scan[...] = lax.fori_loop(first, last, scan, held_scan[...])
-        each(first, last, lambda d: pf_copy(d).start())
-
-        @pl.when((r >= first) & (r < last))
-        def _():
-            pf_recv[my_side, my_tile] = pf_send[r]
+        lax.fori_loop(begin, end, one_group, 0)
 
     def rounds(before, after):
         def of(done):
@@ -529,24 +530,19 @@
 
         own_scan(of(before), of(after))
 
-    done = ((0, 0, 0, 0), (0, 0, 1, 1), (0, 1, 2, 2), (1, 2, 3, 4), (2, 4, 4, 4), (4, 4, 4, 4))
+    done = ((0, 0, 0, 0), (0, 0, 1, 1), (1, 2, 4, 4), (4, 4, 4, 4))
 
     held_scan[...] = jnp.zeros((8, half), F32)
 
-    @pl.when(jnp.logical_not(edge_late))
-    def _():
-        gate_wide(0)
-
+    gate_wide(0)
+    gate_wide(1)
     rounds(done[0], done[1])
-    gate_wide(1)
-    rounds(done[1], done[2])
     wl_load.wait()
     gate_store(dot(tok[...], wl[...]), pl.ds(wides * WIDE, rest))
+    rounds(done[1], done[2])
+    base = lax.fori_loop(0, spans // 2, within, jnp.zeros((1, SPAN), F32))
     rounds(done[2], done[3])
-    base = lax.fori_loop(0, spans // 2, within, jnp.zeros((1, SPAN), F32))
-    rounds(done[3], done[4])
     lax.fori_loop(spans // 2, spans, within, base)
-    rounds(done[4], done[5])
     pltpu.make_async_copy(wo, wo, load_sem.at[5 + 2 * wides]).wait()
 
     bulk(pf_send.at[pl.ds(0, seqs - 1)], pf_ss.at[0], pf_rs.at[0]).wait_recv()
@@ -587,7 +583,7 @@
             send.at[at],
             recv.at[at],
             ss.at[0],
-            rs.at[0] if rs is own_rs else rs.at[at],
+            rs.at[0] if rs is not comb_rs else rs.at[c // (chunks - 1)],
             r,
             (right, left)[way],
         )
@@ -612,7 +608,6 @@
         for way in range(2):
             at = way * chunks + c
             value = dot(gw[1 + way], wo[at])
-            stream(far_send, far_recv, far_ss, far_rs, c, way).wait_recv()
             comb_send[at] = (value + far_recv[at].astype(F32)).astype(BF16)
             stream(comb_send, comb_recv, comb_ss, comb_rs, c, way).start()
         return carry
@@ -627,6 +622,7 @@
     lax.fori_loop(0, chunks, own_step, 0)
     gated(3, g)
     lax.fori_loop(0, 2 * chunks, mine_step, 0)
+    bulk(far_recv, far_ss.at[0], far_rs.at[0]).wait_recv()
     lax.fori_loop(0, chunks, comb_step, 0)
 
     others = pl.ds(0, seqs - 1)
@@ -636,8 +632,7 @@
 
     @pl.when(r < seqs - 1)
     def _():
-        for edge in edges:
-            edge.wait_send()
+        edge.wait_send()
 
     bulk(sq_recv, sq_ss.at[0], sq_rs.at[0]).wait_send()
     bulk(far_send, far_ss.at[0], far_rs.at[0]).wait_send()
@@ -650,10 +645,12 @@
 
     bulk(own_recv, own_ss.at[0], own_rs.at[0]).wait_recv()
     for c in range(chunks):
-        stream(comb_send, comb_recv, comb_ss, comb_rs, c, 0).wait_recv()
+        if c == 0:
+            bulk(comb_recv.at[pl.ds(0, 2 * chunks - 2)], comb_ss.at[0], comb_rs.at[0]).wait_recv()
+        if c == chunks - 1:
+            bulk(comb_recv.at[pl.ds(0, 2)], comb_ss.at[0], comb_rs.at[1]).wait_recv()
         value = mine[c] + own_recv[chunks + c].astype(F32) + comb_recv[c].astype(F32)
         out[:, pl.ds(c * CHUNK, CHUNK)] = (value * scale).astype(BF16)
-        stream(comb_send, comb_recv, comb_ss, comb_rs, c, 1).wait_recv()
         value = mine[chunks + c] + own_recv[c].astype(F32) + comb_recv[chunks + c].astype(F32)
         out[:, pl.ds((chunks + c) * CHUNK, CHUNK)] = (value * scale).astype(BF16)
 
@@ -733,7 +730,7 @@
         pltpu.VMEM((3, 8, SPAN), F32),
         dma((6 + 2 * (width // WIDE),)),
         dma((8,)),
-        dma((2 + 2 * (width // WIDE),)),
+        dma((2,)),
         dma((1,)),
         dma((4,)),
         dma((1,)),
@@ -741,11 +738,11 @@
         dma((1,)),
         dma((1,)),
         dma((1,)),
-        dma((2 * chunks,)),
-        dma((1,)),
-        dma((1,)),
-        dma((1,)),
-        dma((2 * chunks,)),
+        dma((1,)),
+        dma((1,)),
+        dma((1,)),
+        dma((1,)),
+        dma((2,)),
         dma((1,)),
         dma((1,)),
     ]

time: 52.3 us -> 51.9 us (level)
  no operation moved by 1% of the time
where the time goes in v7:
time: 51.9 us; the launch traced here: 51.8 us
  Pallas kernels  51 us (98%)
  local copies, waits for them, and re-layouts  0.84 us (2%)
    pallas_call x1, Pallas kernels, per_device(): pl.pallas_call(functools.partial(kernel, seqs, parts, float(parts * width...  51 us

profile of v7, /device:TPU:1, one launch (start us, length us, event | category | flops | bytes accessed | tf_op | source)
XLA Modules:
  0.0 51.8 jit_solution(11586117360945222525)
XLA Ops:
  0.0 51.0 %shard_map.136 = bf16[128,2560]{1,0:T(8,128)(2,1)S(1)} custom-call(bf16[512,2560]{1,0:T(8,128)(2,1)} %tokens_hbm.1, bf16[2560,1280]{1,0:T(8,128)(2,1)} %wi_hbm.1, bf16[2560,1280]{1,0:T(8,128)(2,1)} %wg_hbm.1, bf16[2560,256]{1,0:T(8,128)(2,1)} %wbc_hbm.1, bf16[20,2560]{1,0:T(8,128)(2,1)} %bitcast.5, f32[4,1280]{1,0:T(4,128)} %conv_i_hbm.1, ...), custom_call_target="tpu_custom_call" | custom-call | tf_op jit(solution)/shard_map/pallas_call | solution.py:750
  51.0 0.8 %copy.16 = bf16[128,2560]{1,0:T(8,128)(2,1)} copy(bf16[128,2560]{1,0:T(8,128)(2,1)S(1)} %shard_map.136) | data formatting | bytes 1310720

commit v8 on v7

--- a/solution.py
+++ b/solution.py
@@ -319,9 +319,9 @@
     group = seqs // 4
     row = r // group
 
-    def dec_copy(dst):
+    def dec_copy(side, chip):
         return far_copy(
-            dec_send.at[lax.rem(dst, 2)], dec_recv.at[r], dec_ss.at[0], dec_rs.at[row], dst, g
+            dec_send.at[side], dec_recv.at[r], dec_ss.at[0], dec_rs.at[row], chip * 2 + side, g
         )
 
     def st_copy(side, chip):
@@ -356,7 +356,8 @@
             act(side, jnp.where(chip >= chips, chip - chips, chip))
             return carry
 
-        lax.fori_loop(1, chips, one, 0)
+        for i in range(1, chips):
+            one(i, 0)
 
         @pl.when(my_side != side)
         def _():
@@ -373,7 +374,8 @@
             jnp.broadcast_to(total[:, 2 * p : 2 * p + 1], (1, SPAN)),
             jnp.broadcast_to(total[:, 2 * p + 1 : 2 * p + 2], (1, SPAN)),
         )
-    each(0, seqs, lambda d: dec_copy(d).start())
+    for side in range(2):
+        to_side(side, lambda at, chip: dec_copy(at, chip).start())
     dec_recv[r] = dec_send[my_side]
 
     def conv(q, j, taps, offset, col, dst, blocks):
@@ -423,14 +425,15 @@
     upper = range(middle + 1, rows // BLOCK)
     lower = range(1, middle + 1)
     per_part = WIDE // SPAN
+    later = convs.pop(1)
     raw_part(0, 0)
     for args in convs:
         conv(*args, upper)
     for q in range(1, 1 + wides):
         raw_part(q, 0)
-        for args in convs[(q - 1) * per_part : q * per_part]:
+        for args in convs[max((q - 1) * per_part - 1, 0) : q * per_part - 1]:
             conv(*args, lower)
-    for args in convs[wides * per_part :]:
+    for args in convs[wides * per_part - 1 :]:
         conv(*args, lower)
 
     @pl.when(r == 0)
@@ -447,6 +450,7 @@
         wt_ref[k] = bc_ref[pl.ds(k * SPAN, SPAN), pl.ds(0, STATE)].astype(F32).T.astype(BF16)
     for col in order:
         local_state(col)
+    conv(*later, range(rows // BLOCK))
 
     def within(k, carry):
         at = pl.ds(pl.multiple_of(k * SPAN, SPAN), SPAN)

time: 51.9 us -> 51.5 us (level)
  no operation moved by 1% of the time
where the time goes in v8:
time: 51.5 us; the launch traced here: 51.4 us
  Pallas kernels  50.5 us (98%)
  local copies, waits for them, and re-layouts  0.84 us (2%)
    pallas_call x1, Pallas kernels, per_device(): pl.pallas_call(functools.partial(kernel, seqs, parts, float(parts * width...  50.5 us

profile of v8, /device:TPU:1, one launch (start us, length us, event | category | flops | bytes accessed | tf_op | source)
XLA Modules:
  0.0 51.4 jit_solution(4111005634933906706)
XLA Ops:
  0.0 50.5 %shard_map.136 = bf16[128,2560]{1,0:T(8,128)(2,1)S(1)} custom-call(bf16[512,2560]{1,0:T(8,128)(2,1)} %tokens_hbm.1, bf16[2560,1280]{1,0:T(8,128)(2,1)} %wi_hbm.1, bf16[2560,1280]{1,0:T(8,128)(2,1)} %wg_hbm.1, bf16[2560,256]{1,0:T(8,128)(2,1)} %wbc_hbm.1, bf16[20,2560]{1,0:T(8,128)(2,1)} %bitcast.5, f32[4,1280]{1,0:T(4,128)} %conv_i_hbm.1, ...), custom_call_target="tpu_custom_call" | custom-call | tf_op jit(solution)/shard_map/pallas_call | solution.py:754
  50.5 0.8 %copy.16 = bf16[128,2560]{1,0:T(8,128)(2,1)} copy(bf16[128,2560]{1,0:T(8,128)(2,1)S(1)} %shard_map.136) | data formatting | bytes 1310720

commit v9 on v8

--- a/solution.py
+++ b/solution.py
@@ -191,29 +191,25 @@
             )
         )
     ]
-    for copy in small_load:
-        copy.start()
     tok_load.start()
     wst_load.start()
-    wbc_load.start()
-    wr_load.start()
 
     barrier = pltpu.get_barrier_semaphore()
 
-    def greet_seq(i, carry):
+    for i in range(1, seqs):
+        peer = jnp.where(r + i >= seqs, r + i - seqs, r + i)
         pl.semaphore_signal(
-            barrier,
-            inc=1,
-            device_id={"seq": lax.rem(r + i, seqs), "head": g},
-            device_id_type=MESH,
-        )
-        return carry
-
-    lax.fori_loop(1, seqs, greet_seq, 0)
+            barrier, inc=1, device_id={"seq": peer, "head": g}, device_id_type=MESH
+        )
     for other in (right, left, across):
         pl.semaphore_signal(
             barrier, inc=1, device_id={"seq": r, "head": other}, device_id_type=MESH
         )
+
+    for copy in small_load:
+        copy.start()
+    wbc_load.start()
+    wr_load.start()
 
     def far_copy(src, dst, ss, rs, seq, head):
         return pltpu.make_async_remote_copy(
@@ -534,7 +530,7 @@
 
         own_scan(of(before), of(after))
 
-    done = ((0, 0, 0, 0), (0, 0, 1, 1), (1, 2, 4, 4), (4, 4, 4, 4))
+    done = ((0, 0, 0, 0), (0, 0, 1, 2), (1, 2, 4, 4), (4, 4, 4, 4))
 
     held_scan[...] = jnp.zeros((8, half), F32)
 

time: 51.5 us -> 51.5 us (level)
  no operation moved by 1% of the time
where the time goes in v9:
time: 51.5 us; the launch traced here: 51.4 us
  Pallas kernels  50.6 us (98%)
  local copies, waits for them, and re-layouts  0.84 us (2%)
    pallas_call x1, Pallas kernels, per_device(): pl.pallas_call(functools.partial(kernel, seqs, parts, float(parts * width...  50.6 us

profile of v9, /device:TPU:1, one launch (start us, length us, event | category | flops | bytes accessed | tf_op | source)
XLA Modules:
  0.0 51.4 jit_solution(17042896130977443059)
XLA Ops:
  0.0 50.6 %shard_map.136 = bf16[128,2560]{1,0:T(8,128)(2,1)S(1)} custom-call(bf16[512,2560]{1,0:T(8,128)(2,1)} %tokens_hbm.1, bf16[2560,1280]{1,0:T(8,128)(2,1)} %wi_hbm.1, bf16[2560,1280]{1,0:T(8,128)(2,1)} %wg_hbm.1, bf16[2560,256]{1,0:T(8,128)(2,1)} %wbc_hbm.1, bf16[20,2560]{1,0:T(8,128)(2,1)} %bitcast.5, f32[4,1280]{1,0:T(4,128)} %conv_i_hbm.1, ...), custom_call_target="tpu_custom_call" | custom-call | tf_op jit(solution)/shard_map/pallas_call | solution.py:750
  50.6 0.8 %copy.16 = bf16[128,2560]{1,0:T(8,128)(2,1)} copy(bf16[128,2560]{1,0:T(8,128)(2,1)S(1)} %shard_map.136) | data formatting | bytes 1310720

commit v10 on v8

--- a/solution.py
+++ b/solution.py
@@ -13,7 +13,7 @@
 SPAN = 128
 HALO = 8
 CHUNK = 256
-BLOCK = 64
+BLOCK = 32
 WIDE = 512
 PIECES = 4
 LOG2E = 1.4426950408889634

time: 51.5 us -> 51.5 us (level)
  no operation moved by 1% of the time
where the time goes in v10:
time: 51.5 us; the launch traced here: 51.4 us
  Pallas kernels  50.5 us (98%)
  local copies, waits for them, and re-layouts  0.84 us (2%)
    pallas_call x1, Pallas kernels, per_device(): pl.pallas_call(functools.partial(kernel, seqs, parts, float(parts * width...  50.5 us

profile of v10, /device:TPU:1, one launch (start us, length us, event | category | flops | bytes accessed | tf_op | source)
XLA Modules:
  0.0 51.4 jit_solution(16008316649712797968)
XLA Ops:
  0.0 50.5 %shard_map.136 = bf16[128,2560]{1,0:T(8,128)(2,1)S(1)} custom-call(bf16[512,2560]{1,0:T(8,128)(2,1)} %tokens_hbm.1, bf16[2560,1280]{1,0:T(8,128)(2,1)} %wi_hbm.1, bf16[2560,1280]{1,0:T(8,128)(2,1)} %wg_hbm.1, bf16[2560,256]{1,0:T(8,128)(2,1)} %wbc_hbm.1, bf16[20,2560]{1,0:T(8,128)(2,1)} %bitcast.5, f32[4,1280]{1,0:T(4,128)} %conv_i_hbm.1, ...), custom_call_target="tpu_custom_call" | custom-call | tf_op jit(solution)/shard_map/pallas_call | solution.py:754
  50.5 0.8 %copy.16 = bf16[128,2560]{1,0:T(8,128)(2,1)} copy(bf16[128,2560]{1,0:T(8,128)(2,1)S(1)} %shard_map.136) | data formatting | bytes 1310720
